TPU v7x, 32 devices: a whole 2x2x4 slice. The times are simulated.
32 devices in a mesh: sess: 16 (over z, x, core), exp: 2 (over y).
Axes of the slice: x: 2, y: 2, z: 4, core: 2. Of those that a mesh axis runs over, the one named last changes fastest.
Arguments:
- tokens: bfloat16 [16, 64, 4096], P('sess'), may hold values from -6 to 6
- routes: int32 [16, 64, 2], P('sess'), may hold values from 0 to 15, all different within a row; in each aligned block of 64 rows (0 to 63, 64 to 127, ..., all dimensions but the last counted through in order) at most 16 rows name the same one
- gates: float32 [16, 64, 2], P('sess'), may hold values from 0.2 to 1
- w_gate: bfloat16 [16, 4096, 1408], P('sess', None, 'exp'), may hold values from -0.09375 to 0.09375
- w_up: bfloat16 [16, 4096, 1408], P('sess', None, 'exp'), may hold values from -0.09375 to 0.09375
- w_down: bfloat16 [16, 1408, 4096], P('sess', 'exp'), may hold values from -0.15625 to 0.15625
- feat_gain: float32 [4096], replicated, may hold values from 0.25 to 1.75
- w_proj: bfloat16 [4096, 256], replicated, may hold values from -0.09375 to 0.09375
- conv_time: bfloat16 [3, 3, 3, 256, 256], replicated, may hold values from -0.078125 to 0.078125
- bias_time: float32 [256], replicated, may hold values from -3 to 3
- conv_space: bfloat16 [3, 3, 256, 256], replicated, may hold values from -0.125 to 0.125
- bias_space: float32 [256], replicated, may hold values from -3 to 3
- frame_cache: bfloat16 [3, 16, 16, 16, 256], P(None, 'sess', 'exp'), may hold values from -6 to 6
- cache_head: int32 [16], P('sess'), may hold values from 0 to 2
Outputs:
- out_frame: bfloat16 [16, 16, 16, 256], P('sess', 'exp')
Inputs may be any that keep to these rules, and one draw needn't show every extreme that they name: `routes`: each token names 2 different experts; among the tokens of one session no expert is named more than 16 times, and in some sessions one is named exactly 16 times. The frame before the previous one is in slot (cache_head + 2) mod 3.
All inputs are finite; a program needn't handle non-finite values.
Results may differ from a plain program's by a relative error of at most 0.017.
Values may be sent and summed in bfloat16 or wider, within the bound.
A program may use at most 64 MiB of HBM per device.

v0:
```python
import functools

import jax
import jax.numpy as jnp
from jax import lax
from jax.experimental import pallas as pl
from jax.experimental.pallas import tpu as pltpu
from jax.sharding import PartitionSpec as P

TOPK = 2
GRID_W = 8
HALO = 2
DIRECT = 4
MESH = pl.DeviceIdType.MESH
VMEM = pl.BlockSpec(memory_space=pltpu.VMEM)

epsilon = 1e-06


def partner(me, bits):
    other, weight = me, 1
    while bits:
        if bits & 1:
            other = other + weight * (1 - 2 * ((me // weight) % 2))
        bits //= 2
        weight *= 2
    return other


def exchange_order(count):
    near = min(4, count)
    order = [k for k in range(1, near)]
    for low in range(near):
        for high in range(count // near - 1, 0, -1):
            order.append(high * near + low)
    return order


def enter(me, tile, sessions, tiles):
    barrier = pltpu.get_barrier_semaphore()
    for k in range(1, sessions):
        pl.semaphore_signal(barrier, inc=1, device_id=(partner(me, k), tile), device_id_type=MESH)
    for m in range(1, tiles):
        pl.semaphore_signal(
            barrier, inc=1, device_id=(me, (tile + m) % tiles), device_id_type=MESH
        )
    pl.semaphore_wait(barrier, sessions - 1 + tiles - 1)


def silu(value):
    return value / (1.0 + jnp.exp(-value))


def across(left, right):
    return lax.dot_general(
        left, right, (((1,), (1,)), ((), ())), preferred_element_type=jnp.float32
    )


def dispatch_kernel(
    sessions,
    tiles,
    cap,
    src,
    past,
    w_gate,
    w_up,
    w_down,
    answer,
    halo,
    out,
    gate_w,
    up_w,
    down_w,
    gate,
    upward,
    hidden,
    own_sem,
    load_sem,
    halo_send,
    halo_recv,
    send1,
    recv1,
    send2,
    recv2,
):
    me, tile = lax.axis_index("sess"), lax.axis_index("exp")
    width = src.shape[1]
    part = width // tiles
    columns = pl.ds(pl.multiple_of(tile * part, part), part)

    def rows(index):
        return pl.ds(pl.multiple_of(index * cap, cap), cap)

    loads = [
        pltpu.make_async_copy(source, held, load_sem.at[i])
        for i, (source, held) in enumerate(
            ((w_gate, gate_w), (w_up, up_w), (w_down, down_w))
        )
    ]
    for load in loads:
        load.start()
    enter(me, tile, sessions, tiles)
    own = pltpu.make_async_copy(src.at[rows(me), :], out.at[rows(me), :], own_sem)
    own.start()
    order = exchange_order(sessions)
    copies = {}
    for k in order:
        other = partner(me, k)
        span = slice(None) if k < DIRECT else columns
        copies[k] = pltpu.make_async_remote_copy(
            src_ref=src.at[rows(other), span],
            dst_ref=out.at[rows(me), span],
            send_sem=send1.at[k],
            recv_sem=recv1.at[k],
            device_id=(other, tile),
            device_id_type=MESH,
        )
        copies[k].start()
    height = past.shape[1]
    borders = []
    for side, begin, step in ((0, height - HALO, 1), (1, 0, tiles - 1)):
        borders.append(
            pltpu.make_async_remote_copy(
                src_ref=past.at[:, begin : begin + HALO],
                dst_ref=halo.at[side],
                send_sem=halo_send.at[side],
                recv_sem=halo_recv.at[side],
                device_id=(me, (tile + step) % tiles),
                device_id_type=MESH,
            )
        )
        borders[-1].start()
    for k in order:
        copies[k].wait_recv()
        if k < DIRECT:
            continue
        block = out.at[rows(partner(me, k)), columns]
        for m in range(1, tiles):
            pltpu.make_async_remote_copy(
                src_ref=block,
                dst_ref=block,
                send_sem=send2.at[m],
                recv_sem=recv2.at[m],
                device_id=(me, (tile + m) % tiles),
                device_id_type=MESH,
            ).start()
    for k in order:
        copies[k].wait_send()
    own.wait()
    passed = out.at[pl.ds(0, (sessions - DIRECT) * cap), columns]
    for m in range(1, tiles):
        pltpu.make_async_copy(passed, passed, send2.at[m]).wait()
        pltpu.make_async_copy(passed, passed, recv2.at[m]).wait()
    for copy in borders:
        copy.wait()
    for load in loads:
        load.wait()
    depth = width // 4
    gate[...] = jnp.zeros_like(gate)
    upward[...] = jnp.zeros_like(upward)

    @pl.loop(0, width // depth)
    def _(step):
        span = pl.ds(pl.multiple_of(step * depth, depth), depth)
        block = out[:, span]
        gate[...] += across(block, gate_w[:, span])
        upward[...] += across(block, up_w[:, span])

    hidden[...] = (silu(gate[...]) * upward[...]).astype(jnp.bfloat16)
    piece = width // 8

    @pl.loop(0, width // piece)
    def _(step):
        span = pl.ds(pl.multiple_of(step * piece, piece), piece)
        answer[:, span] = jnp.dot(
            hidden[...], down_w[:, span], preferred_element_type=jnp.float32
        ).astype(jnp.bfloat16)


def return_kernel(
    sessions,
    tiles,
    cap,
    answer,
    mix_hi,
    mix_lo,
    all_tokens,
    gain,
    all_proj,
    out,
    tokens,
    w_proj,
    load_sem,
    stage,
    reduced,
    back,
    mine,
    theirs,
    send_a,
    recv_a,
    send_b,
    recv_b,
    send_c,
    recv_c,
):
    me, tile = lax.axis_index("sess"), lax.axis_index("exp")
    width = answer.shape[1]
    part = width // tiles
    channels = w_proj.shape[1]

    def rows(index):
        return pl.ds(pl.multiple_of(index * cap, cap), cap)

    def columns(index, offset=0, size=part):
        return pl.ds(pl.multiple_of(index * part + offset, 128), size)

    loads = [
        pltpu.make_async_copy(all_tokens.at[:, columns(tile)], tokens, load_sem.at[0]),
        pltpu.make_async_copy(all_proj.at[columns(tile), :], w_proj, load_sem.at[1]),
    ]
    for load in loads:
        load.start()
    enter(me, tile, sessions, tiles)
    order = exchange_order(sessions)
    order = [k for k in order if k >= 4] + [k for k in order if k < 4] + [0]
    arrivals = {}
    for k in order:
        other = partner(me, k)
        for m in range(1, tiles):
            peer = (tile + m) % tiles
            arrivals[m, k] = pltpu.make_async_remote_copy(
                src_ref=answer.at[rows(other), columns(peer)],
                dst_ref=stage.at[m - 1, rows(other), :],
                send_sem=send_a.at[m],
                recv_sem=recv_a.at[m, k],
                device_id=(me, peer),
                device_id_type=MESH,
            )
            arrivals[m, k].start()
    returns = {}
    for k in order:
        other = partner(me, k)
        total = answer[rows(other), columns(tile)].astype(jnp.float32)
        for m in range(1, tiles):
            arrivals[m, k].wait_recv()
            total = total + stage[m - 1, rows(other), :].astype(jnp.float32)
        if k == 0:
            back[rows(me), :] = total.astype(jnp.bfloat16)
            continue
        reduced[rows(other), :] = total.astype(jnp.bfloat16)
        returns[k] = pltpu.make_async_remote_copy(
            src_ref=reduced.at[rows(other), :],
            dst_ref=back.at[rows(me), :],
            send_sem=send_b.at[k],
            recv_sem=recv_b.at[k],
            device_id=(other, tile),
            device_id_type=MESH,
        )
        returns[k].start()
    for k in order[:-1]:
        returns[k].wait_recv()
    for load in loads:
        load.wait()
    step = min(512, part)
    square = jnp.zeros((tokens.shape[0], 1), jnp.float32)
    coarse = jnp.zeros((tokens.shape[0], channels), jnp.float32)
    for begin in range(0, part, step):
        block = back[:, begin : begin + step]
        mixed = jnp.dot(mix_hi[...], block, preferred_element_type=jnp.float32) + jnp.dot(
            mix_lo[...], block, preferred_element_type=jnp.float32
        )
        span = columns(tile, begin, step)
        here = slice(begin, begin + step)
        feat = (tokens[:, here].astype(jnp.float32) + mixed).astype(jnp.bfloat16)
        feat = feat.astype(jnp.float32)
        square = square + jnp.sum(feat * feat, axis=1, keepdims=True)
        scaled = (feat * gain[:, span]).astype(jnp.bfloat16)
        coarse = coarse + jnp.dot(scaled, w_proj[here, :], preferred_element_type=jnp.float32)
    mine[:, :channels] = coarse
    mine[:, channels:] = jnp.broadcast_to(square, (tokens.shape[0], 128))
    sums = []
    for m in range(1, tiles):
        sums.append(
            pltpu.make_async_remote_copy(
                src_ref=mine,
                dst_ref=theirs.at[m - 1],
                send_sem=send_c.at[m],
                recv_sem=recv_c.at[m],
                device_id=(me, (tile + m) % tiles),
                device_id_type=MESH,
            )
        )
        sums[-1].start()
    for m, copy in enumerate(sums):
        copy.wait_recv()
        coarse = coarse + theirs[m, :, :channels]
        square = square + theirs[m, :, channels : channels + 1]
    out[...] = (coarse * lax.rsqrt(square * (1.0 / width) + epsilon)).astype(jnp.bfloat16).astype(
        jnp.float32
    )
    for copy in sums:
        copy.wait_send()
    for k in order[:-1]:
        returns[k].wait_send()
    for m in range(1, tiles):
        sent = stage.at[m - 1]
        pltpu.make_async_copy(sent, sent, send_a.at[m]).wait()


def route_kernel(
    sessions,
    cap,
    all_routes,
    all_gates,
    all_tokens,
    head,
    cache,
    outgoing,
    mix_hi,
    mix_lo,
    past,
    routes,
    gates,
    tokens,
    sems,
):
    count = tokens.shape[0]
    slots = sessions * cap
    loads = [
        pltpu.make_async_copy(source, held, sems.at[i])
        for i, (source, held) in enumerate(
            (
                (all_routes, routes),
                (all_gates, gates),
                (all_tokens, tokens),
                (cache.at[head[0]], past.at[1]),
                (cache.at[lax.rem(head[0] + 2, 3)], past.at[0]),
            )
        )
    ]
    for load in loads:
        load.start()
    for load in loads:
        load.wait()
    expert = lax.broadcasted_iota(jnp.int32, (sessions, count), 0)
    named = [(routes[k : k + 1, :] == expert).astype(jnp.float32) for k in range(TOPK)]
    earlier = lax.broadcasted_iota(jnp.int32, (count, count), 0) < lax.broadcasted_iota(
        jnp.int32, (count, count), 1
    )
    before = jnp.dot(
        sum(named).astype(jnp.bfloat16),
        earlier.astype(jnp.float32).astype(jnp.bfloat16),
        preferred_element_type=jnp.float32,
    )
    slot = lax.broadcasted_iota(jnp.int32, (slots, count), 0)
    onehot = jnp.zeros((slots, count), jnp.float32)
    weight = jnp.zeros((slots, count), jnp.float32)
    for k in range(TOPK):
        place = jnp.sum(before * named[k], axis=0, keepdims=True).astype(jnp.int32)
        hit = slot == routes[k : k + 1, :] * cap + place
        onehot = onehot + jnp.where(hit, 1.0, 0.0)
        weight = weight + jnp.where(hit, gates[k : k + 1, :], 0.0)
        before = before + named[k]
    weight = weight.T
    high = weight.astype(jnp.bfloat16)
    mix_hi[...] = high
    mix_lo[...] = (weight - high.astype(jnp.float32)).astype(jnp.bfloat16)
    onehot = onehot.astype(jnp.bfloat16)
    step = 512
    for begin in range(0, tokens.shape[1], step):
        outgoing[:, begin : begin + step] = jnp.dot(
            onehot, tokens[:, begin : begin + step], preferred_element_type=jnp.float32
        ).astype(jnp.bfloat16)


def route(routes, gates, tokens, head, cache, sessions, cap):
    slots, count = sessions * cap, tokens.shape[0]
    mix = jax.ShapeDtypeStruct((count, slots), jnp.bfloat16)
    hbm = pl.BlockSpec(memory_space=pltpu.HBM)
    return pl.pallas_call(
        functools.partial(route_kernel, sessions, cap),
        out_shape=(
            jax.ShapeDtypeStruct((slots, tokens.shape[1]), jnp.bfloat16),
            mix,
            mix,
            jax.ShapeDtypeStruct((2,) + cache.shape[1:], cache.dtype),
        ),
        in_specs=[hbm, hbm, hbm, pl.BlockSpec(memory_space=pltpu.SMEM), hbm],
        out_specs=(VMEM,) * 4,
        scratch_shapes=[
            pltpu.VMEM(routes.shape, routes.dtype),
            pltpu.VMEM(gates.shape, gates.dtype),
            pltpu.VMEM(tokens.shape, tokens.dtype),
            pltpu.SemaphoreType.DMA((5,)),
        ],
        compiler_params=pltpu.CompilerParams(vmem_limit_bytes=56 * 2**20),
        name="route",
    )(routes, gates, tokens, head, cache)


def conv_kernel(
    coarse,
    past,
    halo,
    w_time,
    bias_time,
    w_space,
    bias_space,
    out,
    above,
    frames,
    wide,
    wide_active,
):
    tile, tiles = lax.axis_index("exp"), lax.axis_size("exp")
    tall, channels = frames.shape[1:]
    breadth = 2 * GRID_W
    edge = HALO * breadth
    count = out.shape[0]
    grid_rows = coarse.shape[0] // GRID_W
    own_rows = grid_rows // tiles

    for r in range(own_rows + 2):
        row = tile * own_rows - 1 + r
        at = jnp.clip(row, 0, grid_rows - 1)
        value = coarse[pl.ds(pl.multiple_of(at * GRID_W, GRID_W), GRID_W), :]
        above[r * GRID_W : (r + 1) * GRID_W, :] = jnp.where(
            (row >= 0) & (row < grid_rows), value, jnp.zeros_like(value)
        )
    for t in range(2):
        top, bottom = halo[0, t], halo[1, t]
        frames[t, :edge, :] = jnp.where(tile > 0, top, jnp.zeros_like(top))
        frames[t, edge : edge + count, :] = past[t]
        frames[t, edge + count :, :] = jnp.where(
            tile < tiles - 1, bottom, jnp.zeros_like(bottom)
        )

    def chosen(mask):
        return jnp.where(mask, 1.0, 0.0).astype(jnp.bfloat16)

    def moved(matrix, value):
        return jnp.dot(matrix, value, preferred_element_type=jnp.float32).astype(jnp.bfloat16)

    few = above.shape[0]
    pixel = lax.broadcasted_iota(jnp.int32, (tall, few), 0)
    token = lax.broadcasted_iota(jnp.int32, (tall, few), 1)
    spread = chosen(token == (pixel // (2 * breadth)) * GRID_W + (pixel % breadth) // 2)
    frames[2] = moved(spread, above[...].astype(jnp.bfloat16))

    def shifts(size):
        to = lax.broadcasted_iota(jnp.int32, (size, size), 0)
        origin = lax.broadcasted_iota(jnp.int32, (size, size), 1)
        column = to % breadth
        return (
            chosen((origin == to - 1) & (column > 0)),
            chosen((origin == to + 1) & (column < breadth - 1)),
        )

    left, right = shifts(tall)
    for t in range(3):
        wide[t, :, :channels] = moved(left, frames[t])
        wide[t, :, channels : 2 * channels] = frames[t]
        wide[t, :, 2 * channels :] = moved(right, frames[t])
    extended = count + 2 * breadth
    first = jnp.zeros((extended, channels), jnp.float32) + bias_time[...]
    for t in range(3):
        for dy in range(3):
            first = first + jnp.dot(
                wide[t, dy * breadth : dy * breadth + extended, :],
                w_time[3 * t + dy],
                preferred_element_type=jnp.float32,
            )
    row = tile * (count // breadth) - 1 + lax.broadcasted_iota(
        jnp.int32, (extended, channels), 0
    ) // breadth
    inside = (row >= 0) & (row < tiles * (count // breadth))
    active = jnp.where(inside, silu(first), 0.0).astype(jnp.bfloat16)
    left, right = shifts(extended)
    wide_active[:, :channels] = moved(left, active)
    wide_active[:, channels : 2 * channels] = active
    wide_active[:, 2 * channels :] = moved(right, active)
    total = frames[2, edge : edge + count, :].astype(jnp.float32) + bias_space[...]
    for dy in range(3):
        total = total + jnp.dot(
            wide_active[dy * breadth : dy * breadth + count, :],
            w_space[dy],
            preferred_element_type=jnp.float32,
        )
    out[...] = total.astype(jnp.bfloat16)


def decode(coarse, past, halo, w_time, bias_time, w_space, bias_space, tiles):
    count, channels = past.shape[1:]
    breadth = 2 * GRID_W
    tall = count + 2 * HALO * breadth
    few = coarse.shape[0] // tiles + 2 * GRID_W
    return pl.pallas_call(
        conv_kernel,
        out_shape=jax.ShapeDtypeStruct((count, channels), jnp.bfloat16),
        in_specs=[VMEM] * 7,
        out_specs=VMEM,
        scratch_shapes=[
            pltpu.VMEM((few, channels), jnp.float32),
            pltpu.VMEM((3, tall, channels), jnp.bfloat16),
            pltpu.VMEM((3, tall, 3 * channels), jnp.bfloat16),
            pltpu.VMEM((count + 2 * breadth, 3 * channels), jnp.bfloat16),
        ],
        compiler_params=pltpu.CompilerParams(vmem_limit_bytes=24 * 2**20),
        name="decode",
    )(coarse, past, halo, w_time, bias_time, w_space, bias_space)


def dispatch(outgoing, past, w_gate, w_up, w_down, sessions, tiles, cap):
    slots, (hid, width) = outgoing.shape[0], w_gate.shape
    hbm = pl.BlockSpec(memory_space=pl.ANY)
    return pl.pallas_call(
        functools.partial(dispatch_kernel, sessions, tiles, cap),
        out_shape=(
            jax.ShapeDtypeStruct(outgoing.shape, outgoing.dtype),
            jax.ShapeDtypeStruct((2, 2, HALO) + past.shape[2:], past.dtype),
        ),
        in_specs=[VMEM, VMEM, hbm, hbm, hbm],
        out_specs=(VMEM, VMEM),
        scratch_shapes=[
            pltpu.VMEM(outgoing.shape, outgoing.dtype),
            pltpu.VMEM((hid, width), jnp.bfloat16),
            pltpu.VMEM((hid, width), jnp.bfloat16),
            pltpu.VMEM((hid, width), jnp.bfloat16),
            pltpu.VMEM((slots, hid), jnp.float32),
            pltpu.VMEM((slots, hid), jnp.float32),
            pltpu.VMEM((slots, hid), jnp.bfloat16),
            pltpu.SemaphoreType.DMA,
            pltpu.SemaphoreType.DMA((3,)),
            pltpu.SemaphoreType.DMA((2,)),
            pltpu.SemaphoreType.DMA((2,)),
            pltpu.SemaphoreType.DMA((sessions,)),
            pltpu.SemaphoreType.DMA((sessions,)),
            pltpu.SemaphoreType.DMA((tiles,)),
            pltpu.SemaphoreType.DMA((tiles,)),
        ],
        compiler_params=pltpu.CompilerParams(
            collective_id=0, has_side_effects=True, vmem_limit_bytes=50 * 2**20
        ),
        name="dispatch",
    )(outgoing, past, w_gate, w_up, w_down)


def bring_back(answer, mix_hi, mix_lo, tokens, gain, w_proj, sessions, tiles, cap):
    slots, width = answer.shape
    part = width // tiles
    count, channels = tokens.shape[0], w_proj.shape[1]
    return pl.pallas_call(
        functools.partial(return_kernel, sessions, tiles, cap),
        out_shape=jax.ShapeDtypeStruct((count, channels), jnp.float32),
        in_specs=[
            VMEM,
            VMEM,
            VMEM,
            pl.BlockSpec(memory_space=pl.ANY),
            VMEM,
            pl.BlockSpec(memory_space=pl.ANY),
        ],
        out_specs=VMEM,
        scratch_shapes=[
            pltpu.VMEM((count, part), jnp.bfloat16),
            pltpu.VMEM((part, channels), jnp.bfloat16),
            pltpu.SemaphoreType.DMA((2,)),
            pltpu.VMEM((tiles - 1, slots, part), jnp.bfloat16),
            pltpu.VMEM((slots, part), jnp.bfloat16),
            pltpu.VMEM((slots, part), jnp.bfloat16),
            pltpu.VMEM((count, channels + 128), jnp.float32),
            pltpu.VMEM((tiles - 1, count, channels + 128), jnp.float32),
            pltpu.SemaphoreType.DMA((tiles,)),
            pltpu.SemaphoreType.DMA((tiles, sessions)),
            pltpu.SemaphoreType.DMA((sessions,)),
            pltpu.SemaphoreType.DMA((sessions,)),
            pltpu.SemaphoreType.DMA((tiles,)),
            pltpu.SemaphoreType.DMA((tiles,)),
        ],
        compiler_params=pltpu.CompilerParams(
            collective_id=1, has_side_effects=True, vmem_limit_bytes=45 * 2**20
        ),
        name="bring_back",
    )(answer, mix_hi, mix_lo, tokens, gain, w_proj)


def body(
    tokens,
    routes,
    gates,
    w_gate,
    w_up,
    w_down,
    feat_gain,
    w_proj,
    conv_time,
    bias_time,
    conv_space,
    bias_space,
    frame_cache,
    cache_head,
):
    sessions, tiles = lax.axis_size("sess"), lax.axis_size("exp")
    channels = w_proj.shape[-1]
    local = tokens[0]
    tok_count = local.shape[0]
    cap = 2 * tok_count * TOPK // sessions
    height, breadth = frame_cache.shape[2:4]
    outgoing, mix_hi, mix_lo, past = route(
        routes[0].T, gates[0].T, local, cache_head, frame_cache[:, 0], sessions, cap
    )
    answer, halo = dispatch(
        outgoing, past, w_gate[0].T, w_up[0].T, w_down[0], sessions, tiles, cap
    )
    coarse = bring_back(
        answer, mix_hi, mix_lo, local, feat_gain[None, :], w_proj, sessions, tiles, cap
    )
    result = decode(
        coarse,
        past.reshape(2, height * breadth, channels),
        halo.reshape(2, 2, HALO * breadth, channels),
        conv_time.reshape(9, 3 * channels, channels),
        bias_time[None, :],
        conv_space.reshape(3, 3 * channels, channels),
        bias_space[None, :],
        tiles,
    )
    return result.reshape(1, height, breadth, channels)


def solution(mesh):
    return jax.shard_map(
        body,
        mesh=mesh,
        in_specs=(
            P("sess", None, None),
            P("sess", None, None),
            P("sess", None, None),
            P("sess", None, "exp"),
            P("sess", None, "exp"),
            P("sess", "exp", None),
            P(),
            P(),
            P(),
            P(),
            P(),
            P(),
            P(None, "sess", "exp", None, None),
            P("sess"),
        ),
        out_specs=P("sess", "exp", None, None),
        check_vma=False,
    )
```

profile of v0, /device:TPU:0, one launch (start us, length us, event | category | flops | bytes accessed | tf_op | source)
XLA Modules:
  0.0 91.2 jit_solution(17459193407938283942)
XLA Ops:
  0.7 3.3 %route.1 = (bf16[256,4096]{1,0:T(8,128)(2,1)}, bf16[64,256]{1,0:T(8,128)(2,1)}, bf16[64,256]{1,0:T(8,128)(2,1)}, bf16[2,8,16,256]{3,2,1,0:T(8,128)(2,1)}) custom-call(s32[2,64]{1,0:T(2,128)} %bitcast.36, f32[2,64]{1,0:T(2,128)} %bitcast.37, bf16[64,4096]{1,0:T(8,128)(2,1)} %bitcast.24, s32[1]{0:T(128)S(6)} %copy.15.head, bf16[3,8,16,256]{3,2,1,0:T(8,128)(2,1)} %bitcast.35), custom_call_target="tpu_custom_call" | custom-call | tf_op jit(solution)/shard_map/route/pallas_call | solution.py:381
  3.9 0.0 copy-start.4
  4.0 0.9 copy-done.4
  4.8 0.0 copy-start.1
  4.9 0.0 copy-start.2
  4.9 0.0 copy-start.6
  4.9 0.0 copy-start.7
  4.9 0.0 copy-start.8
  4.9 47.7 %dispatch.1 = (bf16[256,4096]{1,0:T(8,128)(2,1)S(1)}, bf16[2,2,2,16,256]{4,3,2,1,0:T(8,128)(2,1)S(1)}) custom-call(bf16[256,4096]{1,0:T(8,128)(2,1)} %get-tuple-element.11.src, bf16[2,8,16,256]{3,2,1,0:T(8,128)(2,1)S(1)} %copy-done.4, bf16[704,4096]{1,0:T(8,128)(2,1)} %bitcast.32, bf16[704,4096]{1,0:T(8,128)(2,1)} %bitcast.33, bf16[704,4096]{1,0:T(8,128)(2,1)} %bitcast.34), custom_call_target="tpu_custom_call" | custom-call | tf_op jit(solution)/shard_map/dispatch/pallas_call | solution.py:517
  52.6 0.0 copy-start
  52.6 0.0 copy-start.3
  52.6 0.0 copy-start.5
  52.6 0.0 copy-start.9
  52.7 0.0 copy-start.10
  52.7 0.0 copy-done.1
  52.7 0.0 copy-done.2
  52.7 0.0 copy-done.6
  52.7 0.0 copy-done.7
  52.7 0.0 copy-done.8
  52.7 35.9 %bring_back.1.coarse = f32[64,256]{1,0:T(8,128)S(1)} custom-call(bf16[256,4096]{1,0:T(8,128)(2,1)S(1)} %get-tuple-element.13.answer, bf16[64,256]{1,0:T(8,128)(2,1)S(1)} %copy-done.6, bf16[64,256]{1,0:T(8,128)(2,1)S(1)} %copy-done.7, bf16[64,4096]{1,0:T(8,128)(2,1)S(1)} %bitcast.25, f32[1,4096]{1,0:T(1,128)S(1)} %bitcast.29, bf16[4096,256]{1,0:T(8,128)(2,1)S(1)} %copy-done.1), custom_call_target="tpu_custom_call" | custom-call | tf_op jit(solution)/shard_map/bring_back/pallas_call | solution.py:553
  88.6 0.0 copy-done
  88.6 0.0 copy-done.3
  88.6 0.0 copy-done.5
  88.6 0.0 copy-done.9
  88.6 0.0 copy-done.10
  88.7 2.5 %decode.1 = bf16[128,256]{1,0:T(8,128)(2,1)} custom-call(f32[64,256]{1,0:T(8,128)S(1)} %bring_back.1.coarse, bf16[2,128,256]{2,1,0:T(8,128)(2,1)S(1)} %bitcast.27, bf16[2,2,32,256]{3,2,1,0:T(8,128)(2,1)S(1)} %bitcast.28, bf16[9,768,256]{2,1,0:T(8,128)(2,1)S(1)} %bitcast.23, f32[1,256]{1,0:T(1,128)S(1)} %bitcast.30, bf16[3,768,256]{2,1,0:T(8,128)(2,1)S(1)} %bitcast.26, ...), custom_call_target="tpu_custom_call" | custom-call | tf_op jit(solution)/shard_map/decode/pallas_call | solution.py:498
Async XLA Ops:
  3.9 0.9 copy-start.4
  4.8 47.8 %copy-start.1 = (bf16[4096,256]{1,0:T(8,128)(2,1)S(1)}, bf16[4096,256]{1,0:T(8,128)(2,1)}, u32[]{:S(2)}) copy-start(bf16[4096,256]{1,0:T(8,128)(2,1)} %all_proj.1) | copy-start | bytes 6291460
  4.9 47.8 %copy-start.2 = (bf16[1,64,4096]{2,1,0:T(8,128)(2,1)S(1)}, bf16[1,64,4096]{2,1,0:T(8,128)(2,1)}, u32[]{:S(2)}) copy-start(bf16[1,64,4096]{2,1,0:T(8,128)(2,1)} %param.14) | copy-start | bytes 1572868
  4.9 47.8 %copy-start.6 = (bf16[64,256]{1,0:T(8,128)(2,1)S(1)}, bf16[64,256]{1,0:T(8,128)(2,1)}, u32[]{:S(2)}) copy-start(bf16[64,256]{1,0:T(8,128)(2,1)} %get-tuple-element.14.mix_hi) | copy-start | bytes 98308
  4.9 47.8 %copy-start.7 = (bf16[64,256]{1,0:T(8,128)(2,1)S(1)}, bf16[64,256]{1,0:T(8,128)(2,1)}, u32[]{:S(2)}) copy-start(bf16[64,256]{1,0:T(8,128)(2,1)} %get-tuple-element.15.mix_lo) | copy-start | bytes 98308
  4.9 47.8 %copy-start.8 = (f32[4096]{0:T(1024)S(1)}, f32[4096]{0:T(1024)}, u32[]{:S(2)}) copy-start(f32[4096]{0:T(1024)} %param.20) | copy-start | bytes 49156
  52.6 36.0 %copy-start = (bf16[3,3,3,256,256]{4,3,2,1,0:T(8,128)(2,1)S(1)}, bf16[3,3,3,256,256]{4,3,2,1,0:T(8,128)(2,1)}, u32[]{:S(2)}) copy-start(bf16[3,3,3,256,256]{4,3,2,1,0:T(8,128)(2,1)} %param.22) | copy-start | bytes 10616836
  52.6 36.0 %copy-start.3 = (bf16[3,3,256,256]{3,2,1,0:T(8,128)(2,1)S(1)}, bf16[3,3,256,256]{3,2,1,0:T(8,128)(2,1)}, u32[]{:S(2)}) copy-start(bf16[3,3,256,256]{3,2,1,0:T(8,128)(2,1)} %param.24) | copy-start | bytes 3538948
  52.6 36.0 %copy-start.5 = (bf16[2,8,16,256]{3,2,1,0:T(8,128)(2,1)S(1)}, bf16[2,8,16,256]{3,2,1,0:T(8,128)(2,1)}, u32[]{:S(2)}) copy-start(bf16[2,8,16,256]{3,2,1,0:T(8,128)(2,1)} %get-tuple-element.12.past) | copy-start | bytes 393220
  52.6 36.0 %copy-start.9 = (f32[256]{0:T(256)S(1)}, f32[256]{0:T(256)}, u32[]{:S(2)}) copy-start(f32[256]{0:T(256)} %param.23) | copy-start | bytes 3076
  52.7 36.0 %copy-start.10 = (f32[256]{0:T(256)S(1)}, f32[256]{0:T(256)}, u32[]{:S(2)}) copy-start(f32[256]{0:T(256)} %param.25) | copy-start | bytes 3076
where the time goes:
time: 91.3 us; the launch traced here: 91.2 us
  Pallas kernels  89.4 us (98%)
  local copies, waits for them, and re-layouts  0.95 us (1%)
    pallas_call x1, Pallas kernels, dispatch(): pl.pallas_call(functools.partial(dispatch_kernel, sessions, tiles, cap),...  47.7 us
    pallas_call x1, Pallas kernels, bring_back(): pl.pallas_call(functools.partial(return_kernel, sessions, tiles, cap), ou...  35.9 us
    pallas_call x1, Pallas kernels, route(): pl.pallas_call(functools.partial(route_kernel, sessions, cap), out_shape=...  3.28 us
    pallas_call x1, Pallas kernels, decode(): pl.pallas_call(conv_kernel, out_shape=jax.ShapeDtypeStruct((count, channe...  2.49 us

commit v1 on v0

v1 whole, which is shorter than its diff:
```python
import functools

import jax
import jax.numpy as jnp
from jax import lax
from jax.experimental import pallas as pl
from jax.experimental.pallas import tpu as pltpu
from jax.sharding import PartitionSpec as P

TOPK = 2
GRID_W = 8
HALO = 2
DIRECT = 4
MESH = pl.DeviceIdType.MESH
VMEM = pl.BlockSpec(memory_space=pltpu.VMEM)

epsilon = 1e-06


def partner(me, bits):
    other, weight = me, 1
    while bits:
        if bits & 1:
            other = other + weight * (1 - 2 * ((me // weight) % 2))
        bits //= 2
        weight *= 2
    return other


def silu(value):
    return value / (1.0 + jnp.exp(-value))


def across(left, right):
    return lax.dot_general(
        left, right, (((1,), (1,)), ((), ())), preferred_element_type=jnp.float32
    )


def pieces_of(part):
    unit = max(128, part // 8)
    sizes, left = [], part // unit
    while left > 0:
        take = 2 if left > 2 else 1
        sizes.append(take * unit)
        left -= take
    starts = [sum(sizes[:i]) for i in range(len(sizes))]
    return list(zip(starts, sizes))


def expert_kernel(
    sessions,
    tiles,
    cap,
    pieces,
    all_routes,
    all_gates,
    head,
    all_gain,
    all_tokens,
    w_gate,
    w_up,
    w_down,
    all_proj,
    all_cache,
    out,
    past,
    halo,
    routes,
    gates,
    gain,
    tokens,
    gate_w,
    up_w,
    down_w,
    w_proj,
    cache,
    near_hot,
    far_hot,
    near_mix,
    far_mix,
    hot_in,
    mix_in,
    relay_in,
    near_out,
    relay_out,
    rows_in,
    gate,
    upward,
    hidden,
    answer,
    stage,
    reduced,
    back,
    partial,
    summed,
    mine,
    theirs,
    load_sem,
    halo_sem,
    table_sem,
    token_sem,
    near_sem,
    far_sem,
    cross_sem,
    answer_sem,
    own_sem,
    other_sem,
    sum_sem,
    last_sem,
):
    me, tile = lax.axis_index("sess"), lax.axis_index("exp")
    half = sessions // 2
    direct = min(DIRECT, half)
    upper, h = me // half, me % half
    far = partner(me, half)
    span = half * cap
    part = rows_in.shape[2]
    width = part * tiles
    count, channels = tokens.shape[1], w_proj.shape[1]
    turns = range(len(pieces))

    def rows(index, base=0):
        return pl.ds(pl.multiple_of(base + index * cap, cap), cap)

    def peer(k):
        return partner(me, k), partner(h, k)

    def piece(j):
        begin, size = pieces[j]
        return slice(begin, begin + size)

    def remote(source, target, sems, where, device):
        return pltpu.make_async_remote_copy(
            src_ref=source,
            dst_ref=target,
            send_sem=sems.at[(0,) + where],
            recv_sem=sems.at[(1,) + where],
            device_id=device,
            device_id_type=MESH,
        )

    def drain(block, sems, where):
        pltpu.make_async_copy(block, block, sems.at[where]).wait()

    small = [
        pltpu.make_async_copy(all_routes, routes, load_sem.at[0]),
        pltpu.make_async_copy(all_gates, gates, load_sem.at[1]),
        pltpu.make_async_copy(all_cache, cache, load_sem.at[2]),
    ]
    token_loads = [
        pltpu.make_async_copy(
            all_tokens.at[:, m * part : (m + 1) * part], tokens.at[m], load_sem.at[3 + m]
        )
        for m in range(tiles)
    ]
    begin = pl.multiple_of(tile * part, part)
    big = [
        pltpu.make_async_copy(source, held, load_sem.at[3 + tiles + i])
        for i, (source, held) in enumerate(
            (
                (w_gate, gate_w),
                (w_up, up_w),
                (w_down, down_w),
                (all_proj.at[pl.ds(begin, part), :], w_proj),
                (all_gain.at[:, pl.ds(begin, part)], gain),
            )
        )
    ]
    for load in small + token_loads + big:
        load.start()

    barrier = pltpu.get_barrier_semaphore()
    for k in range(1, half + 1):
        pl.semaphore_signal(barrier, inc=1, device_id=(partner(me, k), tile), device_id_type=MESH)
    for m in range(1, tiles):
        pl.semaphore_signal(
            barrier, inc=1, device_id=(me, (tile + m) % tiles), device_id_type=MESH
        )

    small[0].wait()
    small[1].wait()
    expert = lax.broadcasted_iota(jnp.int32, (sessions, count), 0)
    named = [(routes[k : k + 1, :] == expert).astype(jnp.float32) for k in range(TOPK)]
    earlier = lax.broadcasted_iota(jnp.int32, (count, count), 0) < lax.broadcasted_iota(
        jnp.int32, (count, count), 1
    )
    before = jnp.dot(
        sum(named).astype(jnp.bfloat16),
        earlier.astype(jnp.float32).astype(jnp.bfloat16),
        preferred_element_type=jnp.float32,
    )
    targets = []
    for k in range(TOPK):
        place = jnp.sum(before * named[k], axis=0, keepdims=True).astype(jnp.int32)
        targets.append(routes[k : k + 1, :] * cap + place)
        before = before + named[k]
    for base, hot, mix in (
        (upper * span, near_hot, near_mix),
        ((1 - upper) * span, far_hot, far_mix),
    ):
        slot = base + lax.broadcasted_iota(jnp.int32, (span, count), 0)
        onehot = jnp.zeros((span, count), jnp.float32)
        weight = jnp.zeros((span, count), jnp.float32)
        for k in range(TOPK):
            hit = slot == targets[k]
            onehot = onehot + jnp.where(hit, 1.0, 0.0)
            weight = weight + jnp.where(hit, gates[k : k + 1, :], 0.0)
        weight = weight.T
        high = weight.astype(jnp.bfloat16)
        hot[...] = onehot.astype(jnp.bfloat16)
        mix[0] = high
        mix[1] = (weight - high.astype(jnp.float32)).astype(jnp.bfloat16)
    small[2].wait()
    chosen = head[0]
    frames = [cache[i] for i in range(3)]
    for t, shift in ((1, 0), (0, 2)):
        which = lax.rem(chosen + shift, 3)
        past[t] = jnp.where(which == 0, frames[0], jnp.where(which == 1, frames[1], frames[2]))
    for load in token_loads:
        load.wait()
    pl.semaphore_wait(barrier, half + tiles - 1)

    pending = [
        remote(far_hot, hot_in, table_sem, (0,), (far, tile)),
        remote(far_mix, mix_in, table_sem, (1,), (far, tile)),
    ]
    pending[0].start()
    near, relayed = {}, []
    for j in turns:
        here = piece(j)
        relayed.append(
            remote(
                tokens.at[tile, :, here], relay_in.at[:, here], token_sem, (j,), (far, tile)
            )
        )
        relayed[j].start()
        for m in range(tiles):
            near_out[m, :, here] = jnp.dot(
                near_hot[...], tokens[m, :, here], preferred_element_type=jnp.float32
            ).astype(jnp.bfloat16)
        for k in range(half - 1, 0, -1):
            other, index = peer(k)
            if k < direct:
                source, target = near_out.at[:, rows(index), here], rows_in.at[:, rows(h), here]
            else:
                source = near_out.at[tile, rows(index), here]
                target = rows_in.at[tile, rows(h), here]
            near[k, j] = remote(source, target, near_sem, (k, j), (other, tile))
            near[k, j].start()
        rows_in[:, rows(h), here] = near_out[:, rows(h), here]
    pending[1].start()
    height = past.shape[1]
    for side, first, step in ((0, height - HALO, 1), (1, 0, tiles - 1)):
        pending.append(
            remote(
                past.at[:, first : first + HALO],
                halo.at[side],
                halo_sem,
                (side,),
                (me, (tile + step) % tiles),
            )
        )
        pending[-1].start()
    pending[0].wait_recv()
    for load in big:
        load.wait()
    gate[...] = jnp.zeros_like(gate)
    upward[...] = jnp.zeros_like(upward)
    distant = {}

    def relay(j):
        here = piece(j)
        relayed[j].wait_recv()
        relay_out[:, here] = jnp.dot(
            hot_in[...], relay_in[:, here], preferred_element_type=jnp.float32
        ).astype(jnp.bfloat16)
        for k in range(half - 1, 0, -1):
            other, index = peer(k)
            distant[k, j] = remote(
                relay_out.at[rows(index), here],
                rows_in.at[tile, rows(h, span), here],
                far_sem,
                (k, j),
                (other, tile),
            )
            distant[k, j].start()
        rows_in[tile, rows(h, span), here] = relay_out[rows(h), here]

    def cross(j):
        here = piece(j)

        def forward(block):
            for m in range(1, tiles):
                remote(block, block, cross_sem, (m, j), (me, (tile + m) % tiles)).start()

        forward(rows_in.at[tile, rows(h, span), here])
        for k in range(direct, half):
            near[k, j].wait_recv()
            forward(rows_in.at[tile, rows(peer(k)[1]), here])
        for k in range(1, half):
            distant[k, j].wait_recv()
            forward(rows_in.at[tile, rows(peer(k)[1], span), here])

    def passed(j):
        return rows_in.at[0, pl.ds(0, (2 * half - direct) * cap), piece(j)]

    def consume(j):
        start, size = pieces[j]
        here = piece(j)
        for k in range(1, direct):
            near[k, j].wait_recv()
        for m in range(1, tiles):
            drain(passed(j), cross_sem, (1, m, j))

        @pl.loop(0, tiles)
        def _(m):
            span_in = pl.ds(pl.multiple_of(m * part + start, 128), size)
            block = rows_in[m, :, here]
            gate[...] += across(block, gate_w[:, span_in])
            upward[...] += across(block, up_w[:, span_in])

    for j in range(len(pieces) + 2):
        if j < len(pieces):
            relay(j)
        if 0 <= j - 1 < len(pieces):
            cross(j - 1)
        if 0 <= j - 2:
            consume(j - 2)
    hidden[...] = (silu(gate[...]) * upward[...]).astype(jnp.bfloat16)

    def project(m, j):
        start, size = pieces[j]
        span_in = pl.ds(pl.multiple_of(m * part + start, 128), size)
        return jnp.dot(hidden[...], down_w[:, span_in], preferred_element_type=jnp.float32)

    arrivals = {}
    for j in turns:
        here = piece(j)
        for m in range(1, tiles):
            to = (tile + m) % tiles
            answer[m - 1, :, here] = project(to, j).astype(jnp.bfloat16)
            arrivals[m, j] = remote(
                answer.at[m - 1, :, here], stage.at[m - 1, :, here], answer_sem, (m, j), (me, to)
            )
            arrivals[m, j].start()
    owns, others, sums = {}, {}, []

    def reduce(j):
        here = piece(j)
        total = project(tile, j)
        for m in range(1, tiles):
            arrivals[m, j].wait_recv()
            total = total + stage[m - 1, :, here].astype(jnp.float32)
        reduced[:, here] = total.astype(jnp.bfloat16)
        for k in range(half - 1, 0, -1):
            other, index = peer(k)
            for base, sems, made in ((span, other_sem, others), (0, own_sem, owns)):
                made[k, j] = remote(
                    reduced.at[rows(index, base), here],
                    back.at[rows(h, base), here],
                    sems,
                    (k, j),
                    (other, tile),
                )
                made[k, j].start()
        for base in (0, span):
            back[rows(h, base), here] = reduced[rows(h, base), here]

    def blend(mix, base, here):
        block = back[base : base + span, here]
        return jnp.dot(mix[0], block, preferred_element_type=jnp.float32) + jnp.dot(
            mix[1], block, preferred_element_type=jnp.float32
        )

    def give(j):
        here = piece(j)
        for k in range(1, half):
            others[k, j].wait_recv()
        if j == 0:
            pending[1].wait_recv()
        partial[:, here] = blend(mix_in, span, here).astype(jnp.bfloat16)
        sums.append(
            remote(partial.at[:, here], summed.at[:, here], sum_sem, (j,), (far, tile))
        )
        sums[j].start()

    square = jnp.zeros((count, 1), jnp.float32)
    coarse = jnp.zeros((count, channels), jnp.float32)
    for j in range(len(pieces) + 2):
        if j < len(pieces):
            reduce(j)
        if 0 <= j - 1 < len(pieces):
            give(j - 1)
        if 0 <= j - 2:
            here = piece(j - 2)
            for k in range(1, half):
                owns[k, j - 2].wait_recv()
            mixed = blend(near_mix, 0, here)
            sums[j - 2].wait_recv()
            mixed = mixed + summed[:, here].astype(jnp.float32)
            feat = (tokens[tile, :, here].astype(jnp.float32) + mixed).astype(jnp.bfloat16)
            feat = feat.astype(jnp.float32)
            square = square + jnp.sum(feat * feat, axis=1, keepdims=True)
            scaled = (feat * gain[:, here]).astype(jnp.bfloat16)
            coarse = coarse + jnp.dot(
                scaled, w_proj[here, :], preferred_element_type=jnp.float32
            )
    mine[:, :channels] = coarse
    mine[:, channels:] = jnp.broadcast_to(square, (count, 128))
    totals = []
    for m in range(1, tiles):
        totals.append(
            remote(mine, theirs.at[m - 1], last_sem, (m,), (me, (tile + m) % tiles))
        )
        totals[-1].start()
    for m, copy in enumerate(totals):
        copy.wait_recv()
        coarse = coarse + theirs[m, :, :channels]
        square = square + theirs[m, :, channels : channels + 1]
    out[...] = (coarse * lax.rsqrt(square * (1.0 / width) + epsilon)).astype(jnp.bfloat16).astype(
        jnp.float32
    )

    for copy in pending + relayed + sums + totals:
        copy.wait_send()
    for copy in pending[2:]:
        copy.wait_recv()
    for made in (near, distant, owns, others, arrivals):
        for copy in made.values():
            copy.wait_send()
    for j in turns:
        for m in range(1, tiles):
            drain(passed(j), cross_sem, (0, m, j))


def experts(routes, gates, head, gain, tokens, w_gate, w_up, w_down, w_proj, cache, sizes):
    sessions, tiles, cap = sizes
    count, width = tokens.shape
    hid, part, half = w_gate.shape[0], width // tiles, sessions // 2
    span, channels = half * cap, w_proj.shape[1]
    pieces = pieces_of(part)
    hbm = pl.BlockSpec(memory_space=pltpu.HBM)
    low, full = jnp.bfloat16, jnp.float32
    turns = len(pieces)
    return pl.pallas_call(
        functools.partial(expert_kernel, sessions, tiles, cap, pieces),
        out_shape=(
            jax.ShapeDtypeStruct((count, channels), full),
            jax.ShapeDtypeStruct((2,) + cache.shape[1:], cache.dtype),
            jax.ShapeDtypeStruct((2, 2, HALO) + cache.shape[2:], cache.dtype),
        ),
        in_specs=[hbm, hbm, pl.BlockSpec(memory_space=pltpu.SMEM)] + [hbm] * 7,
        out_specs=(VMEM,) * 3,
        scratch_shapes=[
            pltpu.VMEM(routes.shape, routes.dtype),
            pltpu.VMEM(gates.shape, gates.dtype),
            pltpu.VMEM((1, part), full),
            pltpu.VMEM((tiles, count, part), low),
            pltpu.VMEM((hid, width), low),
            pltpu.VMEM((hid, width), low),
            pltpu.VMEM((hid, width), low),
            pltpu.VMEM((part, channels), low),
            pltpu.VMEM(cache.shape, low),
            pltpu.VMEM((span, count), low),
            pltpu.VMEM((span, count), low),
            pltpu.VMEM((2, count, span), low),
            pltpu.VMEM((2, count, span), low),
            pltpu.VMEM((span, count), low),
            pltpu.VMEM((2, count, span), low),
            pltpu.VMEM((count, part), low),
            pltpu.VMEM((tiles, span, part), low),
            pltpu.VMEM((span, part), low),
            pltpu.VMEM((tiles, 2 * span, part), low),
            pltpu.VMEM((2 * span, hid), full),
            pltpu.VMEM((2 * span, hid), full),
            pltpu.VMEM((2 * span, hid), low),
            pltpu.VMEM((tiles - 1, 2 * span, part), low),
            pltpu.VMEM((tiles - 1, 2 * span, part), low),
            pltpu.VMEM((2 * span, part), low),
            pltpu.VMEM((2 * span, part), low),
            pltpu.VMEM((count, part), low),
            pltpu.VMEM((count, part), low),
            pltpu.VMEM((count, channels + 128), full),
            pltpu.VMEM((tiles - 1, count, channels + 128), full),
            pltpu.SemaphoreType.DMA((8 + tiles,)),
            pltpu.SemaphoreType.DMA((2, 2)),
            pltpu.SemaphoreType.DMA((2, 2)),
            pltpu.SemaphoreType.DMA((2, turns)),
            pltpu.SemaphoreType.DMA((2, half, turns)),
            pltpu.SemaphoreType.DMA((2, half, turns)),
            pltpu.SemaphoreType.DMA((2, tiles, turns)),
            pltpu.SemaphoreType.DMA((2, tiles, turns)),
            pltpu.SemaphoreType.DMA((2, half, turns)),
            pltpu.SemaphoreType.DMA((2, half, turns)),
            pltpu.SemaphoreType.DMA((2, turns)),
            pltpu.SemaphoreType.DMA((2, tiles)),
        ],
        compiler_params=pltpu.CompilerParams(
            collective_id=0, has_side_effects=True, vmem_limit_bytes=54 * 2**20
        ),
        name="experts",
    )(routes, gates, head, gain, tokens, w_gate, w_up, w_down, w_proj, cache)


def conv_kernel(
    coarse,
    past,
    halo,
    w_time,
    bias_time,
    w_space,
    bias_space,
    out,
    above,
    frames,
    wide,
    wide_active,
):
    tile, tiles = lax.axis_index("exp"), lax.axis_size("exp")
    tall, channels = frames.shape[1:]
    breadth = 2 * GRID_W
    edge = HALO * breadth
    count = out.shape[0]
    grid_rows = coarse.shape[0] // GRID_W
    own_rows = grid_rows // tiles

    for r in range(own_rows + 2):
        row = tile * own_rows - 1 + r
        at = jnp.clip(row, 0, grid_rows - 1)
        value = coarse[pl.ds(pl.multiple_of(at * GRID_W, GRID_W), GRID_W), :]
        above[r * GRID_W : (r + 1) * GRID_W, :] = jnp.where(
            (row >= 0) & (row < grid_rows), value, jnp.zeros_like(value)
        )
    for t in range(2):
        top, bottom = halo[0, t], halo[1, t]
        frames[t, :edge, :] = jnp.where(tile > 0, top, jnp.zeros_like(top))
        frames[t, edge : edge + count, :] = past[t]
        frames[t, edge + count :, :] = jnp.where(
            tile < tiles - 1, bottom, jnp.zeros_like(bottom)
        )

    def chosen(mask):
        return jnp.where(mask, 1.0, 0.0).astype(jnp.bfloat16)

    def moved(matrix, value):
        return jnp.dot(matrix, value, preferred_element_type=jnp.float32).astype(jnp.bfloat16)

    few = above.shape[0]
    pixel = lax.broadcasted_iota(jnp.int32, (tall, few), 0)
    token = lax.broadcasted_iota(jnp.int32, (tall, few), 1)
    spread = chosen(token == (pixel // (2 * breadth)) * GRID_W + (pixel % breadth) // 2)
    frames[2] = moved(spread, above[...].astype(jnp.bfloat16))

    def shifts(size):
        to = lax.broadcasted_iota(jnp.int32, (size, size), 0)
        origin = lax.broadcasted_iota(jnp.int32, (size, size), 1)
        column = to % breadth
        return (
            chosen((origin == to - 1) & (column > 0)),
            chosen((origin == to + 1) & (column < breadth - 1)),
        )

    left, right = shifts(tall)
    for t in range(3):
        wide[t, :, :channels] = moved(left, frames[t])
        wide[t, :, channels : 2 * channels] = frames[t]
        wide[t, :, 2 * channels :] = moved(right, frames[t])
    extended = count + 2 * breadth
    first = jnp.zeros((extended, channels), jnp.float32) + bias_time[...]
    for t in range(3):
        for dy in range(3):
            first = first + jnp.dot(
                wide[t, dy * breadth : dy * breadth + extended, :],
                w_time[3 * t + dy],
                preferred_element_type=jnp.float32,
            )
    row = tile * (count // breadth) - 1 + lax.broadcasted_iota(
        jnp.int32, (extended, channels), 0
    ) // breadth
    inside = (row >= 0) & (row < tiles * (count // breadth))
    active = jnp.where(inside, silu(first), 0.0).astype(jnp.bfloat16)
    left, right = shifts(extended)
    wide_active[:, :channels] = moved(left, active)
    wide_active[:, channels : 2 * channels] = active
    wide_active[:, 2 * channels :] = moved(right, active)
    total = frames[2, edge : edge + count, :].astype(jnp.float32) + bias_space[...]
    for dy in range(3):
        total = total + jnp.dot(
            wide_active[dy * breadth : dy * breadth + count, :],
            w_space[dy],
            preferred_element_type=jnp.float32,
        )
    out[...] = total.astype(jnp.bfloat16)


def decode(coarse, past, halo, w_time, bias_time, w_space, bias_space, tiles):
    count, channels = past.shape[1:]
    breadth = 2 * GRID_W
    tall = count + 2 * HALO * breadth
    few = coarse.shape[0] // tiles + 2 * GRID_W
    return pl.pallas_call(
        conv_kernel,
        out_shape=jax.ShapeDtypeStruct((count, channels), jnp.bfloat16),
        in_specs=[VMEM] * 7,
        out_specs=VMEM,
        scratch_shapes=[
            pltpu.VMEM((few, channels), jnp.float32),
            pltpu.VMEM((3, tall, channels), jnp.bfloat16),
            pltpu.VMEM((3, tall, 3 * channels), jnp.bfloat16),
            pltpu.VMEM((count + 2 * breadth, 3 * channels), jnp.bfloat16),
        ],
        compiler_params=pltpu.CompilerParams(vmem_limit_bytes=24 * 2**20),
        name="decode",
    )(coarse, past, halo, w_time, bias_time, w_space, bias_space)


def body(
    tokens,
    routes,
    gates,
    w_gate,
    w_up,
    w_down,
    feat_gain,
    w_proj,
    conv_time,
    bias_time,
    conv_space,
    bias_space,
    frame_cache,
    cache_head,
):
    sessions, tiles = lax.axis_size("sess"), lax.axis_size("exp")
    channels = w_proj.shape[-1]
    local = tokens[0]
    tok_count = local.shape[0]
    cap = 2 * tok_count * TOPK // sessions
    height, breadth = frame_cache.shape[2:4]
    coarse, past, halo = experts(
        routes[0].T,
        gates[0].T,
        cache_head,
        feat_gain[None, :],
        local,
        w_gate[0].T,
        w_up[0].T,
        w_down[0],
        w_proj,
        frame_cache[:, 0],
        (sessions, tiles, cap),
    )
    result = decode(
        coarse,
        past.reshape(2, height * breadth, channels),
        halo.reshape(2, 2, HALO * breadth, channels),
        conv_time.reshape(9, 3 * channels, channels),
        bias_time[None, :],
        conv_space.reshape(3, 3 * channels, channels),
        bias_space[None, :],
        tiles,
    )
    return result.reshape(1, height, breadth, channels)


def solution(mesh):
    return jax.shard_map(
        body,
        mesh=mesh,
        in_specs=(
            P("sess", None, None),
            P("sess", None, None),
            P("sess", None, None),
            P("sess", None, "exp"),
            P("sess", None, "exp"),
            P("sess", "exp", None),
            P(),
            P(),
            P(),
            P(),
            P(),
            P(),
            P(None, "sess", "exp", None, None),
            P("sess"),
        ),
        out_specs=P("sess", "exp", None, None),
        check_vma=False,
    )
```

time: 91.3 us -> 86.9 us (0.952)
  Pallas kernels: 89.4 us -> 83.4 us
  local copies, waits for them, and re-layouts: 0.95 us -> 2.59 us
    pallas_call x3 -> x1, Pallas kernels: 86.9 us -> 80.9 us  [experts(): pl.pallas_call(functools.partial(expert_kernel, sessions, tiles, cap, pie...]
    unnamed x22 -> x14, local copies, waits for them, and re-layouts: 0.95 us -> 2.59 us
where the time goes in v1:
time: 86.9 us; the launch traced here: 86.7 us
  Pallas kernels  83.4 us (96%)
  local copies, waits for them, and re-layouts  2.59 us (3%)
    pallas_call x1, Pallas kernels, experts(): pl.pallas_call(functools.partial(expert_kernel, sessions, tiles, cap, pie...  80.9 us
    unnamed x14, local copies, waits for them, and re-layouts  2.59 us
    pallas_call x1, Pallas kernels, decode(): pl.pallas_call(conv_kernel, out_shape=jax.ShapeDtypeStruct((count, channe...  2.49 us

profile of v1, /device:TPU:0, one launch (start us, length us, event | category | flops | bytes accessed | tf_op | source)
XLA Modules:
  0.0 86.7 jit_solution(16680723812377648020)
XLA Ops:
  0.7 0.0 copy-start
  0.7 0.0 copy-start.1
  0.7 0.0 copy-start.5
  0.7 0.0 copy-start.6
  0.7 80.9 %experts.1 = (f32[64,256]{1,0:T(8,128)}, bf16[2,8,16,256]{3,2,1,0:T(8,128)(2,1)}, bf16[2,2,2,16,256]{4,3,2,1,0:T(8,128)(2,1)}) custom-call(s32[2,64]{1,0:T(2,128)} %bitcast.35, f32[2,64]{1,0:T(2,128)} %bitcast.36, s32[1]{0:T(128)S(6)} %copy.15.head, f32[1,4096]{1,0:T(1,128)} %bitcast.34, bf16[64,4096]{1,0:T(8,128)(2,1)} %bitcast.32, ...), custom_call_target="tpu_custom_call" | custom-call | tf_op jit(solution)/shard_map/experts/pallas_call | solution.py:446
  81.6 0.0 copy-done
  81.6 0.0 copy-done.1
  81.6 0.0 copy-done.5
  81.6 0.0 copy-done.6
  81.6 0.0 copy-start.2
  81.6 0.9 %copy-done.2 = bf16[2,8,16,256]{3,2,1,0:T(8,128)(2,1)S(1)} copy-done((bf16[2,8,16,256]{3,2,1,0:T(8,128)(2,1)S(1)}, bf16[2,8,16,256]{3,2,1,0:T(8,128)(2,1)}, u32[]{:S(2)}) %copy-start.2) | copy-done | bytes 131096
  82.5 0.0 copy-start.3
  82.5 0.8 copy-done.3
  83.4 0.0 copy-start.4
  83.4 0.8 copy-done.4
  84.2 2.5 %decode.1 = bf16[128,256]{1,0:T(8,128)(2,1)} custom-call(f32[64,256]{1,0:T(8,128)S(1)} %copy-done.3, bf16[2,128,256]{2,1,0:T(8,128)(2,1)S(1)} %bitcast.25, bf16[2,2,32,256]{3,2,1,0:T(8,128)(2,1)S(1)} %bitcast.26, bf16[9,768,256]{2,1,0:T(8,128)(2,1)S(1)} %bitcast.23, f32[1,256]{1,0:T(1,128)S(1)} %bitcast.27, bf16[3,768,256]{2,1,0:T(8,128)(2,1)S(1)} %bitcast.24, ...), custom_call_target="tpu_custom_call" | custom-call | tf_op jit(solution)/shard_map/decode/pallas_call | solution.py:602
Async XLA Ops:
  0.7 80.9 %copy-start = (bf16[3,3,3,256,256]{4,3,2,1,0:T(8,128)(2,1)S(1)}, bf16[3,3,3,256,256]{4,3,2,1,0:T(8,128)(2,1)}, u32[]{:S(2)}) copy-start(bf16[3,3,3,256,256]{4,3,2,1,0:T(8,128)(2,1)} %param.22) | copy-start | bytes 10616836
  0.7 80.9 %copy-start.1 = (bf16[3,3,256,256]{3,2,1,0:T(8,128)(2,1)S(1)}, bf16[3,3,256,256]{3,2,1,0:T(8,128)(2,1)}, u32[]{:S(2)}) copy-start(bf16[3,3,256,256]{3,2,1,0:T(8,128)(2,1)} %param.24) | copy-start | bytes 3538948
  0.7 80.9 %copy-start.5 = (f32[256]{0:T(256)S(1)}, f32[256]{0:T(256)}, u32[]{:S(2)}) copy-start(f32[256]{0:T(256)} %param.23) | copy-start | bytes 3076
  0.7 80.9 %copy-start.6 = (f32[256]{0:T(256)S(1)}, f32[256]{0:T(256)}, u32[]{:S(2)}) copy-start(f32[256]{0:T(256)} %param.25) | copy-start | bytes 3076
  81.6 0.9 %copy-start.2 = (bf16[2,8,16,256]{3,2,1,0:T(8,128)(2,1)S(1)}, bf16[2,8,16,256]{3,2,1,0:T(8,128)(2,1)}, u32[]{:S(2)}) copy-start(bf16[2,8,16,256]{3,2,1,0:T(8,128)(2,1)} %get-tuple-element.9) | copy-start | bytes 393220
  82.5 0.8 copy-start.3
  83.4 0.8 copy-start.4

commit v2 on v1

v2 whole, which is shorter than its diff:
```python
import functools

import jax
import jax.numpy as jnp
from jax import lax
from jax.experimental import pallas as pl
from jax.experimental.pallas import tpu as pltpu
from jax.sharding import PartitionSpec as P

TOPK = 2
GRID_W = 8
HALO = 2
DIRECT = 4
MESH = pl.DeviceIdType.MESH
VMEM = pl.BlockSpec(memory_space=pltpu.VMEM)

epsilon = 1e-06


def partner(me, bits):
    other, weight = me, 1
    while bits:
        if bits & 1:
            other = other + weight * (1 - 2 * ((me // weight) % 2))
        bits //= 2
        weight *= 2
    return other


def silu(value):
    return value / (1.0 + jnp.exp(-value))


def across(left, right):
    return lax.dot_general(
        left, right, (((1,), (1,)), ((), ())), preferred_element_type=jnp.float32
    )


def pieces_of(part):
    unit = max(128, part // 8)
    sizes, left = [], part // unit
    while left > 0:
        take = 2 if left > 2 else 1
        sizes.append(take * unit)
        left -= take
    starts = [sum(sizes[:i]) for i in range(len(sizes))]
    return list(zip(starts, sizes))


def layer_kernel(
    sessions,
    tiles,
    cap,
    pieces,
    all_routes,
    all_gates,
    head,
    all_gain,
    all_tokens,
    w_gate,
    w_up,
    w_down,
    all_proj,
    all_cache,
    all_time,
    all_time_bias,
    all_space,
    all_space_bias,
    out,
    routes,
    gates,
    gain,
    tokens,
    gate_w,
    up_w,
    down_w,
    w_proj,
    cache,
    w_time,
    bias_time,
    w_space,
    bias_space,
    past,
    halo,
    near_hot,
    far_hot,
    near_mix,
    far_mix,
    hot_in,
    mix_in,
    relay_in,
    near_out,
    relay_out,
    rows_in,
    gate,
    upward,
    hidden,
    near_answer,
    near_back,
    near_mixed,
    own_mixed,
    mixed_in,
    answer,
    stage,
    reduced,
    back,
    partial,
    summed,
    mine,
    theirs,
    coarse_in,
    above,
    frames,
    wide,
    first,
    wide_active,
    load_sem,
    halo_sem,
    table_sem,
    token_sem,
    near_sem,
    far_sem,
    near_cross,
    far_cross,
    back_sem,
    mixed_sem,
    answer_sem,
    other_sem,
    sum_sem,
    last_sem,
):
    me, tile = lax.axis_index("sess"), lax.axis_index("exp")
    half = sessions // 2
    direct = min(DIRECT, half)
    upper, h = me // half, me % half
    far = partner(me, half)
    span = half * cap
    part = rows_in.shape[2]
    width = part * tiles
    count, channels = tokens.shape[1], w_proj.shape[1]
    turns = range(len(pieces))

    def rows(index, base=0):
        return pl.ds(pl.multiple_of(base + index * cap, cap), cap)

    def peer(k):
        return partner(me, k), partner(h, k)

    def piece(j):
        begin, size = pieces[j]
        return slice(begin, begin + size)

    def columns(m, j):
        begin, size = pieces[j]
        return pl.ds(pl.multiple_of(m * part + begin, 128), size)

    def remote(source, target, sems, where, device):
        return pltpu.make_async_remote_copy(
            src_ref=source,
            dst_ref=target,
            send_sem=sems.at[(0,) + where],
            recv_sem=sems.at[(1,) + where],
            device_id=device,
            device_id_type=MESH,
        )

    def drain(block, sems, where):
        pltpu.make_async_copy(block, block, sems.at[where]).wait()

    begin = pl.multiple_of(tile * part, part)
    sources = [(all_routes, routes), (all_gates, gates)]
    sources += [
        (all_tokens.at[:, m * part : (m + 1) * part], tokens.at[m]) for m in range(tiles)
    ]
    sources += [
        (all_cache, cache),
        (w_gate, gate_w),
        (w_up, up_w),
        (w_down, down_w),
        (all_time, w_time),
        (all_time_bias, bias_time),
        (all_space, w_space),
        (all_space_bias, bias_space),
        (all_proj.at[pl.ds(begin, part), :], w_proj),
        (all_gain.at[:, pl.ds(begin, part)], gain),
    ]
    loads = [
        pltpu.make_async_copy(source, held, load_sem.at[i])
        for i, (source, held) in enumerate(sources)
    ]
    for load in loads:
        load.start()
    token_loads, loads = loads[: 2 + tiles], loads[2 + tiles :]

    barrier = pltpu.get_barrier_semaphore()
    for k in range(1, half + 1):
        pl.semaphore_signal(barrier, inc=1, device_id=(partner(me, k), tile), device_id_type=MESH)
    for m in range(1, tiles):
        pl.semaphore_signal(
            barrier, inc=1, device_id=(me, (tile + m) % tiles), device_id_type=MESH
        )

    token_loads[0].wait()
    token_loads[1].wait()
    expert = lax.broadcasted_iota(jnp.int32, (sessions, count), 0)
    named = [(routes[k : k + 1, :] == expert).astype(jnp.float32) for k in range(TOPK)]
    earlier = lax.broadcasted_iota(jnp.int32, (count, count), 0) < lax.broadcasted_iota(
        jnp.int32, (count, count), 1
    )
    before = jnp.dot(
        sum(named).astype(jnp.bfloat16),
        earlier.astype(jnp.float32).astype(jnp.bfloat16),
        preferred_element_type=jnp.float32,
    )
    targets = []
    for k in range(TOPK):
        place = jnp.sum(before * named[k], axis=0, keepdims=True).astype(jnp.int32)
        targets.append(routes[k : k + 1, :] * cap + place)
        before = before + named[k]
    weights = []
    for base, hot in ((upper * span, near_hot), ((1 - upper) * span, far_hot)):
        slot = base + lax.broadcasted_iota(jnp.int32, (span, count), 0)
        onehot = jnp.zeros((span, count), jnp.float32)
        weight = jnp.zeros((span, count), jnp.float32)
        for k in range(TOPK):
            hit = slot == targets[k]
            onehot = onehot + jnp.where(hit, 1.0, 0.0)
            weight = weight + jnp.where(hit, gates[k : k + 1, :], 0.0)
        hot[...] = onehot.astype(jnp.bfloat16)
        weights.append(weight)
    for load in token_loads[2:]:
        load.wait()
    pl.semaphore_wait(barrier, half + tiles - 1)

    pending = [remote(far_hot, hot_in, table_sem, (0,), (far, tile))]
    pending[0].start()
    relayed = [
        remote(
            tokens.at[tile, :, piece(j)], relay_in.at[:, piece(j)], token_sem, (j,), (far, tile)
        )
        for j in turns
    ]
    relayed[0].start()
    near = {}
    for j in turns:
        here = piece(j)
        for m in range(tiles):
            near_out[m, :, here] = jnp.dot(
                near_hot[...], tokens[m, :, here], preferred_element_type=jnp.float32
            ).astype(jnp.bfloat16)
        for k in range(half - 1, 0, -1):
            other, index = peer(k)
            if k < direct:
                source, target = near_out.at[:, rows(index), here], rows_in.at[:, rows(h), here]
            else:
                source = near_out.at[tile, rows(index), here]
                target = rows_in.at[tile, rows(h), here]
            near[k, j] = remote(source, target, near_sem, (k, j), (other, tile))
            near[k, j].start()
        rows_in[:, rows(h), here] = near_out[:, rows(h), here]
    for copy in relayed[1:]:
        copy.start()
    for weight, mix in zip(weights, (near_mix, far_mix)):
        weight = weight.T
        high = weight.astype(jnp.bfloat16)
        mix[0] = high
        mix[1] = (weight - high.astype(jnp.float32)).astype(jnp.bfloat16)
    pending.append(remote(far_mix, mix_in, table_sem, (1,), (far, tile)))
    pending[1].start()

    loads[0].wait()
    newest = head[0]
    slots = [cache[i] for i in range(3)]
    for t, shift in ((1, 0), (0, 2)):
        which = lax.rem(newest + shift, 3)
        past[t] = jnp.where(which == 0, slots[0], jnp.where(which == 1, slots[1], slots[2]))
    height = past.shape[1]
    for side, start, step in ((0, height - HALO, 1), (1, 0, tiles - 1)):
        pending.append(
            remote(
                past.at[:, start : start + HALO],
                halo.at[side],
                halo_sem,
                (side,),
                (me, (tile + step) % tiles),
            )
        )
        pending[-1].start()

    distant = {}

    def forward(block, sems, j):
        for m in range(1, tiles):
            remote(block, block, sems, (m, j), (me, (tile + m) % tiles)).start()

    def near_forward(j):
        for k in range(direct, half):
            near[k, j].wait_recv()
            forward(rows_in.at[tile, rows(peer(k)[1]), piece(j)], near_cross, j)

    def relay(j):
        here = piece(j)
        if j == 0:
            pending[0].wait_recv()
        relayed[j].wait_recv()
        relay_out[:, here] = jnp.dot(
            hot_in[...], relay_in[:, here], preferred_element_type=jnp.float32
        ).astype(jnp.bfloat16)
        for k in range(half - 1, 0, -1):
            other, index = peer(k)
            distant[k, j] = remote(
                relay_out.at[rows(index), here],
                rows_in.at[tile, rows(h, span), here],
                far_sem,
                (k, j),
                (other, tile),
            )
            distant[k, j].start()
        rows_in[tile, rows(h, span), here] = relay_out[rows(h), here]

    def far_forward(j):
        here = piece(j)
        forward(rows_in.at[tile, rows(h, span), here], far_cross, j)
        for k in range(1, half):
            distant[k, j].wait_recv()
            forward(rows_in.at[tile, rows(peer(k)[1], span), here], far_cross, j)

    def near_passed(j):
        return rows_in.at[0, pl.ds(0, (half - direct) * cap), piece(j)]

    def far_passed(j):
        return rows_in.at[0, pl.ds(0, span), piece(j)]

    def consume(group, j):
        base = group * span
        if group == 0:
            for k in range(1, direct):
                near[k, j].wait_recv()
        for m in range(1, tiles):
            if group == 0:
                drain(near_passed(j), near_cross, (1, m, j))
            else:
                drain(far_passed(j), far_cross, (1, m, j))
        if j == 0:
            gate[...] = jnp.zeros_like(gate)
            upward[...] = jnp.zeros_like(upward)

        @pl.loop(0, tiles)
        def _(m):
            block = rows_in[m, base : base + span, piece(j)]
            gate[...] += across(block, gate_w[:, columns(m, j)])
            upward[...] += across(block, up_w[:, columns(m, j)])

    def activate(group):
        hidden[group] = (silu(gate[...]) * upward[...]).astype(jnp.bfloat16)

    def project(group, m, j):
        return jnp.dot(
            hidden[group], down_w[:, columns(m, j)], preferred_element_type=jnp.float32
        )

    home, tied = {}, {}

    def near_return(j):
        here = piece(j)

        @pl.loop(0, tiles)
        def _(m):
            near_answer[m, :, here] = project(0, m, j).astype(jnp.bfloat16)

        for k in range(half - 1, 0, -1):
            other, index = peer(k)
            home[k, j] = remote(
                near_answer.at[:, rows(index), here],
                near_back.at[:, rows(h), here],
                back_sem,
                (k, j),
                (other, tile),
            )
            home[k, j].start()
        near_back[:, rows(h), here] = near_answer[:, rows(h), here]

    def blend(mix, block):
        return jnp.dot(mix[0], block, preferred_element_type=jnp.float32) + jnp.dot(
            mix[1], block, preferred_element_type=jnp.float32
        )

    def near_blend(j):
        here = piece(j)
        for k in range(1, half):
            home[k, j].wait_recv()
        for m in range(1, tiles):
            to = (tile + m) % tiles
            near_mixed[m - 1, :, here] = blend(near_mix, near_back[to, :, here]).astype(
                jnp.bfloat16
            )
            tied[m, j] = remote(
                near_mixed.at[m - 1, :, here],
                mixed_in.at[m - 1, :, here],
                mixed_sem,
                (m, j),
                (me, to),
            )
            tied[m, j].start()
        own_mixed[:, here] = blend(near_mix, near_back[tile, :, here])

    arrivals, others, sums = {}, {}, []

    def far_answer(j):
        here = piece(j)
        for m in range(1, tiles):
            to = (tile + m) % tiles
            answer[m - 1, :, here] = project(1, to, j).astype(jnp.bfloat16)
            arrivals[m, j] = remote(
                answer.at[m - 1, :, here], stage.at[m - 1, :, here], answer_sem, (m, j), (me, to)
            )
            arrivals[m, j].start()

    def far_return(j):
        here = piece(j)
        total = project(1, tile, j)
        for m in range(1, tiles):
            arrivals[m, j].wait_recv()
            total = total + stage[m - 1, :, here].astype(jnp.float32)
        reduced[:, here] = total.astype(jnp.bfloat16)
        for k in range(half - 1, 0, -1):
            other, index = peer(k)
            others[k, j] = remote(
                reduced.at[rows(index), here],
                back.at[rows(h), here],
                other_sem,
                (k, j),
                (other, tile),
            )
            others[k, j].start()
        back[rows(h), here] = reduced[rows(h), here]

    def far_blend(j):
        here = piece(j)
        if j == 0:
            pending[1].wait_recv()
        for k in range(1, half):
            others[k, j].wait_recv()
        partial[:, here] = blend(mix_in, back[:, here]).astype(jnp.bfloat16)
        sums.append(
            remote(partial.at[:, here], summed.at[:, here], sum_sem, (j,), (far, tile))
        )
        sums[j].start()

    def features(j):
        here = piece(j)
        mixed = own_mixed[:, here]
        for m in range(1, tiles):
            tied[m, j].wait_recv()
            mixed = mixed + mixed_in[m - 1, :, here].astype(jnp.float32)
        sums[j].wait_recv()
        mixed = mixed + summed[:, here].astype(jnp.float32)
        feat = (tokens[tile, :, here].astype(jnp.float32) + mixed).astype(jnp.bfloat16)
        feat = feat.astype(jnp.float32)
        scaled = (feat * gain[:, here]).astype(jnp.bfloat16)
        return (
            jnp.sum(feat * feat, axis=1, keepdims=True),
            jnp.dot(scaled, w_proj[here, :], preferred_element_type=jnp.float32),
        )

    tall = frames.shape[1]
    breadth = 2 * GRID_W
    edge = HALO * breadth
    pixels = out.shape[0]
    extended = pixels + 2 * breadth
    grid_rows = count // GRID_W
    own_rows = grid_rows // tiles

    def chosen(mask):
        return jnp.where(mask, 1.0, 0.0).astype(jnp.bfloat16)

    def moved(matrix, value):
        return jnp.dot(matrix, value, preferred_element_type=jnp.float32).astype(jnp.bfloat16)

    def shifts(size):
        to = lax.broadcasted_iota(jnp.int32, (size, size), 0)
        origin = lax.broadcasted_iota(jnp.int32, (size, size), 1)
        column = to % breadth
        return (
            chosen((origin == to - 1) & (column > 0)),
            chosen((origin == to + 1) & (column < breadth - 1)),
        )

    def widen(t, left, right):
        wide[t, :, :channels] = moved(left, frames[t])
        wide[t, :, channels : 2 * channels] = frames[t]
        wide[t, :, 2 * channels :] = moved(right, frames[t])

    def in_time(t):
        total = jnp.zeros((extended, channels), jnp.float32)
        for dy in range(3):
            total = total + jnp.dot(
                wide[t, dy * breadth : dy * breadth + extended, :],
                w_time[3 * t + dy],
                preferred_element_type=jnp.float32,
            )
        return total

    def earlier_frames():
        for copy in pending[2:]:
            copy.wait_recv()
        left, right = shifts(tall)
        for t in range(2):
            top = halo[0, t].reshape(edge, channels)
            bottom = halo[1, t].reshape(edge, channels)
            frames[t, :edge, :] = jnp.where(tile > 0, top, jnp.zeros_like(top))
            frames[t, edge : edge + pixels, :] = past[t].reshape(pixels, channels)
            frames[t, edge + pixels :, :] = jnp.where(
                tile < tiles - 1, bottom, jnp.zeros_like(bottom)
            )
            widen(t, left, right)
        first[...] = in_time(0) + in_time(1) + bias_time[...]

    def last_frame():
        for r in range(own_rows + 2):
            row = tile * own_rows - 1 + r
            at = jnp.clip(row, 0, grid_rows - 1)
            value = coarse_in[pl.ds(pl.multiple_of(at * GRID_W, GRID_W), GRID_W), :]
            above[r * GRID_W : (r + 1) * GRID_W, :] = jnp.where(
                (row >= 0) & (row < grid_rows), value, jnp.zeros_like(value)
            )
        few = above.shape[0]
        pixel = lax.broadcasted_iota(jnp.int32, (tall, few), 0)
        token = lax.broadcasted_iota(jnp.int32, (tall, few), 1)
        spread = chosen(token == (pixel // (2 * breadth)) * GRID_W + (pixel % breadth) // 2)
        frames[2] = moved(spread, above[...].astype(jnp.bfloat16))
        left, right = shifts(tall)
        widen(2, left, right)
        total = first[...] + in_time(2)
        row = tile * (pixels // breadth) - 1 + lax.broadcasted_iota(
            jnp.int32, (extended, channels), 0
        ) // breadth
        inside = (row >= 0) & (row < tiles * (pixels // breadth))
        active = jnp.where(inside, silu(total), 0.0).astype(jnp.bfloat16)
        left, right = shifts(extended)
        wide_active[:, :channels] = moved(left, active)
        wide_active[:, channels : 2 * channels] = active
        wide_active[:, 2 * channels :] = moved(right, active)
        total = frames[2, edge : edge + pixels, :].astype(jnp.float32) + bias_space[...]
        for dy in range(3):
            total = total + jnp.dot(
                wide_active[dy * breadth : dy * breadth + pixels, :],
                w_space[dy],
                preferred_element_type=jnp.float32,
            )
        out[...] = total.astype(jnp.bfloat16)

    n = len(pieces)

    def steps(*stages):
        reach = n + max(lag for lag, _ in stages)
        for j in range(reach):
            for lag, stage_of in stages:
                if 0 <= j - lag < n:
                    stage_of(j - lag)

    for load in loads[1:3]:
        load.wait()
    steps((0, near_forward), (1, functools.partial(consume, 0)))
    activate(0)
    steps((0, relay), (3, far_forward))
    loads[3].wait()
    steps((0, near_return), (1, functools.partial(consume, 1)))
    activate(1)
    steps((0, far_answer))
    steps((0, near_blend))
    for load in loads[4:]:
        load.wait()
    earlier_frames()
    found = []
    steps((0, far_return), (1, far_blend), (2, lambda j: found.append(features(j))))
    square = sum(pair[0] for pair in found)
    coarse = sum(pair[1] for pair in found)
    lane = lax.broadcasted_iota(jnp.int32, (count, 128), 1)
    high = square.astype(jnp.bfloat16).astype(jnp.float32)
    mine[:, :channels] = coarse.astype(jnp.bfloat16)
    mine[:, channels:] = jnp.where(
        lane == 0, high, jnp.where(lane == 1, square - high, 0.0)
    ).astype(jnp.bfloat16)
    totals = []
    for m in range(1, tiles):
        totals.append(
            remote(mine, theirs.at[m - 1], last_sem, (m,), (me, (tile + m) % tiles))
        )
        totals[-1].start()
    for m, copy in enumerate(totals):
        copy.wait_recv()
        coarse = coarse + theirs[m, :, :channels].astype(jnp.float32)
        square = square + jnp.sum(
            theirs[m, :, channels:].astype(jnp.float32), axis=1, keepdims=True
        )
    coarse_in[...] = coarse * lax.rsqrt(square * (1.0 / width) + epsilon)
    last_frame()

    for copy in pending + relayed + sums + totals:
        copy.wait_send()
    for made in (near, distant, home, tied, others, arrivals):
        for copy in made.values():
            copy.wait_send()
    for j in turns:
        for m in range(1, tiles):
            drain(near_passed(j), near_cross, (0, m, j))
            drain(far_passed(j), far_cross, (0, m, j))


def layer(
    routes,
    gates,
    head,
    gain,
    tokens,
    w_gate,
    w_up,
    w_down,
    w_proj,
    cache,
    w_time,
    bias_time,
    w_space,
    bias_space,
    sizes,
):
    sessions, tiles, cap = sizes
    count, width = tokens.shape
    hid, part, half = w_gate.shape[0], width // tiles, sessions // 2
    span, channels = half * cap, w_proj.shape[1]
    pixels = cache.shape[1] * cache.shape[2]
    breadth = 2 * GRID_W
    tall = pixels + 2 * HALO * breadth
    few = count // tiles + 2 * GRID_W
    pieces = pieces_of(part)
    hbm = pl.BlockSpec(memory_space=pltpu.HBM)
    low, full = jnp.bfloat16, jnp.float32
    n = len(pieces)
    held = [
        (routes.shape, routes.dtype),
        (gates.shape, full),
        ((1, part), full),
        ((tiles, count, part), low),
        (w_gate.shape, low),
        (w_up.shape, low),
        (w_down.shape, low),
        ((part, channels), low),
        (cache.shape, low),
        (w_time.shape, low),
        (bias_time.shape, full),
        (w_space.shape, low),
        (bias_space.shape, full),
        ((2,) + cache.shape[1:], low),
        ((2, 2, HALO) + cache.shape[2:], low),
        ((span, count), low),
        ((span, count), low),
        ((2, count, span), low),
        ((2, count, span), low),
        ((span, count), low),
        ((2, count, span), low),
        ((count, part), low),
        ((tiles, span, part), low),
        ((span, part), low),
        ((tiles, 2 * span, part), low),
        ((span, hid), full),
        ((span, hid), full),
        ((2, span, hid), low),
        ((tiles, span, part), low),
        ((tiles, span, part), low),
        ((tiles - 1, count, part), low),
        ((count, part), full),
        ((tiles - 1, count, part), low),
        ((tiles - 1, span, part), low),
        ((tiles - 1, span, part), low),
        ((span, part), low),
        ((span, part), low),
        ((count, part), low),
        ((count, part), low),
        ((count, channels + 128), low),
        ((tiles - 1, count, channels + 128), low),
        ((count, channels), full),
        ((few, channels), full),
        ((3, tall, channels), low),
        ((3, tall, 3 * channels), low),
        ((pixels + 2 * breadth, channels), full),
        ((pixels + 2 * breadth, 3 * channels), low),
    ]
    sems = [
        (12 + tiles,),
        (2, 2),
        (2, 2),
        (2, n),
        (2, half, n),
        (2, half, n),
        (2, tiles, n),
        (2, tiles, n),
        (2, half, n),
        (2, tiles, n),
        (2, tiles, n),
        (2, half, n),
        (2, n),
        (2, tiles),
    ]
    return pl.pallas_call(
        functools.partial(layer_kernel, sessions, tiles, cap, pieces),
        out_shape=jax.ShapeDtypeStruct((pixels, channels), low),
        in_specs=[hbm, hbm, pl.BlockSpec(memory_space=pltpu.SMEM)] + [hbm] * 11,
        out_specs=VMEM,
        scratch_shapes=[pltpu.VMEM(*each) for each in held]
        + [pltpu.SemaphoreType.DMA(each) for each in sems],
        compiler_params=pltpu.CompilerParams(
            collective_id=0, has_side_effects=True, vmem_limit_bytes=60 * 2**20
        ),
        name="layer",
    )(
        routes,
        gates,
        head,
        gain,
        tokens,
        w_gate,
        w_up,
        w_down,
        w_proj,
        cache,
        w_time,
        bias_time,
        w_space,
        bias_space,
    )


def body(
    tokens,
    routes,
    gates,
    w_gate,
    w_up,
    w_down,
    feat_gain,
    w_proj,
    conv_time,
    bias_time,
    conv_space,
    bias_space,
    frame_cache,
    cache_head,
):
    sessions, tiles = lax.axis_size("sess"), lax.axis_size("exp")
    channels = w_proj.shape[-1]
    local = tokens[0]
    tok_count = local.shape[0]
    cap = 2 * tok_count * TOPK // sessions
    height, breadth = frame_cache.shape[2:4]
    result = layer(
        routes[0].T,
        gates[0].T,
        cache_head,
        feat_gain[None, :],
        local,
        w_gate[0].T,
        w_up[0].T,
        w_down[0],
        w_proj,
        frame_cache[:, 0],
        conv_time.reshape(9, 3 * channels, channels),
        bias_time[None, :],
        conv_space.reshape(3, 3 * channels, channels),
        bias_space[None, :],
        (sessions, tiles, cap),
    )
    return result.reshape(1, height, breadth, channels)


def solution(mesh):
    return jax.shard_map(
        body,
        mesh=mesh,
        in_specs=(
            P("sess", None, None),
            P("sess", None, None),
            P("sess", None, None),
            P("sess", None, "exp"),
            P("sess", None, "exp"),
            P("sess", "exp", None),
            P(),
            P(),
            P(),
            P(),
            P(),
            P(),
            P(None, "sess", "exp", None, None),
            P("sess"),
        ),
        out_specs=P("sess", "exp", None, None),
        check_vma=False,
    )
```

time: 86.9 us -> 82 us (0.944)
  Pallas kernels: 83.4 us -> 79.7 us
  local copies, waits for them, and re-layouts: 2.59 us -> 1.47 us
    pallas_call x2 -> x1, Pallas kernels: 83.4 us -> 79.7 us  [layer(): pl.pallas_call(functools.partial(layer_kernel, sessions, tiles, cap, piec...]
    unnamed x14 -> x1, local copies, waits for them, and re-layouts: 2.59 us -> 1.47 us
where the time goes in v2:
time: 82 us; the launch traced here: 81.9 us
  Pallas kernels  79.7 us (97%)
  local copies, waits for them, and re-layouts  1.47 us (2%)
    pallas_call x1, Pallas kernels, layer(): pl.pallas_call(functools.partial(layer_kernel, sessions, tiles, cap, piec...  79.7 us

profile of v2, /device:TPU:0, one launch (start us, length us, event | category | flops | bytes accessed | tf_op | source)
XLA Modules:
  0.0 81.9 jit_solution(1326220264817812887)
XLA Ops:
  0.7 79.7 %layer.1 = bf16[128,256]{1,0:T(8,128)(2,1)} custom-call(s32[2,64]{1,0:T(2,128)} %bitcast.30, f32[2,64]{1,0:T(2,128)} %bitcast.31, s32[1]{0:T(128)S(6)} %copy.16.head, f32[1,4096]{1,0:T(1,128)} %bitcast.29, bf16[64,4096]{1,0:T(8,128)(2,1)} %bitcast.26, bf16[704,4096]{1,0:T(8,128)(2,1)} %bitcast.21, bf16[704,4096]{1,0:T(8,128)(2,1)} %bitcast.22, ...), custom_call_target="tpu_custom_call" | custom-call | tf_op jit(solution)/shard_map/layer/pallas_call | solution.py:706
  80.4 1.5 %copy.17 = bf16[1,8,16,256]{3,2,1,0:T(8,128)(2,1)} copy(bf16[1,8,16,256]{3,2,1,0:T(8,128)(2,1)} %bitcast.27) | data formatting | bytes 131072

commit v3 on v2

--- a/solution.py
+++ b/solution.py
@@ -38,14 +38,8 @@
 
 
 def pieces_of(part):
-    unit = max(128, part // 8)
-    sizes, left = [], part // unit
-    while left > 0:
-        take = 2 if left > 2 else 1
-        sizes.append(take * unit)
-        left -= take
-    starts = [sum(sizes[:i]) for i in range(len(sizes))]
-    return list(zip(starts, sizes))
+    size = max(128, part // 4)
+    return [(begin, size) for begin in range(0, part, size)]
 
 
 def layer_kernel(
@@ -120,6 +114,7 @@
     table_sem,
     token_sem,
     near_sem,
+    direct_sem,
     far_sem,
     near_cross,
     far_cross,
@@ -139,13 +134,14 @@
     part = rows_in.shape[2]
     width = part * tiles
     count, channels = tokens.shape[1], w_proj.shape[1]
-    turns = range(len(pieces))
+    n = len(pieces)
+    turns = range(n)
 
     def rows(index, base=0):
         return pl.ds(pl.multiple_of(base + index * cap, cap), cap)
 
-    def peer(k):
-        return partner(me, k), partner(h, k)
+    peers = [(partner(me, k), partner(h, k)) for k in range(half)]
+    block_of = [partner(h // direct, b) for b in range(half // direct)]
 
     def piece(j):
         begin, size = pieces[j]
@@ -155,18 +151,24 @@
         begin, size = pieces[j]
         return pl.ds(pl.multiple_of(m * part + begin, 128), size)
 
-    def remote(source, target, sems, where, device):
-        return pltpu.make_async_remote_copy(
+    def send(source, target, sent, arrived, device):
+        pltpu.make_async_remote_copy(
             src_ref=source,
             dst_ref=target,
-            send_sem=sems.at[(0,) + where],
-            recv_sem=sems.at[(1,) + where],
+            send_sem=sent,
+            recv_sem=arrived,
             device_id=device,
             device_id_type=MESH,
-        )
-
-    def drain(block, sems, where):
-        pltpu.make_async_copy(block, block, sems.at[where]).wait()
+        ).start()
+
+    def drain(block, sem):
+        pltpu.make_async_copy(block, block, sem).wait()
+
+    def some(j, number):
+        return rows_in.at[0, pl.ds(0, number * cap), slice(None) if j is None else piece(j)]
+
+    def many(j, number):
+        return rows_in.at[:, pl.ds(0, number * cap), slice(None) if j is None else piece(j)]
 
     begin = pl.multiple_of(tile * part, part)
     sources = [(all_routes, routes), (all_gates, gates)]
@@ -199,6 +201,20 @@
     for m in range(1, tiles):
         pl.semaphore_signal(
             barrier, inc=1, device_id=(me, (tile + m) % tiles), device_id_type=MESH
+        )
+
+    for load in token_loads[2:]:
+        load.wait()
+    pl.semaphore_wait(barrier, half + tiles - 1)
+
+    def hand_over(j):
+        here = piece(j)
+        send(
+            tokens.at[tile, :, here],
+            relay_in.at[:, here],
+            token_sem.at[n],
+            token_sem.at[j],
+            (far, tile),
         )
 
     token_loads[0].wait()
@@ -229,20 +245,7 @@
             weight = weight + jnp.where(hit, gates[k : k + 1, :], 0.0)
         hot[...] = onehot.astype(jnp.bfloat16)
         weights.append(weight)
-    for load in token_loads[2:]:
-        load.wait()
-    pl.semaphore_wait(barrier, half + tiles - 1)
-
-    pending = [remote(far_hot, hot_in, table_sem, (0,), (far, tile))]
-    pending[0].start()
-    relayed = [
-        remote(
-            tokens.at[tile, :, piece(j)], relay_in.at[:, piece(j)], token_sem, (j,), (far, tile)
-        )
-        for j in turns
-    ]
-    relayed[0].start()
-    near = {}
+    send(far_hot, hot_in, table_sem.at[0, 0], table_sem.at[1, 0], (far, tile))
     for j in turns:
         here = piece(j)
         for m in range(tiles):
@@ -250,24 +253,24 @@
                 near_hot[...], tokens[m, :, here], preferred_element_type=jnp.float32
             ).astype(jnp.bfloat16)
         for k in range(half - 1, 0, -1):
-            other, index = peer(k)
+            other, index = peers[k]
             if k < direct:
                 source, target = near_out.at[:, rows(index), here], rows_in.at[:, rows(h), here]
+                sems = direct_sem
             else:
                 source = near_out.at[tile, rows(index), here]
                 target = rows_in.at[tile, rows(h), here]
-            near[k, j] = remote(source, target, near_sem, (k, j), (other, tile))
-            near[k, j].start()
+                sems = near_sem
+            send(source, target, sems.at[n], sems.at[j], (other, tile))
         rows_in[:, rows(h), here] = near_out[:, rows(h), here]
-    for copy in relayed[1:]:
-        copy.start()
+    for j in turns:
+        hand_over(j)
     for weight, mix in zip(weights, (near_mix, far_mix)):
         weight = weight.T
         high = weight.astype(jnp.bfloat16)
         mix[0] = high
         mix[1] = (weight - high.astype(jnp.float32)).astype(jnp.bfloat16)
-    pending.append(remote(far_mix, mix_in, table_sem, (1,), (far, tile)))
-    pending[1].start()
+    send(far_mix, mix_in, table_sem.at[0, 1], table_sem.at[1, 1], (far, tile))
 
     loads[0].wait()
     newest = head[0]
@@ -277,77 +280,62 @@
         past[t] = jnp.where(which == 0, slots[0], jnp.where(which == 1, slots[1], slots[2]))
     height = past.shape[1]
     for side, start, step in ((0, height - HALO, 1), (1, 0, tiles - 1)):
-        pending.append(
-            remote(
-                past.at[:, start : start + HALO],
-                halo.at[side],
-                halo_sem,
-                (side,),
-                (me, (tile + step) % tiles),
-            )
+        send(
+            past.at[:, start : start + HALO],
+            halo.at[side],
+            halo_sem.at[0, side],
+            halo_sem.at[1, side],
+            (me, (tile + step) % tiles),
         )
-        pending[-1].start()
-
-    distant = {}
 
     def forward(block, sems, j):
         for m in range(1, tiles):
-            remote(block, block, sems, (m, j), (me, (tile + m) % tiles)).start()
+            send(block, block, sems.at[m, n], sems.at[m, j], (me, (tile + m) % tiles))
 
     def near_forward(j):
-        for k in range(direct, half):
-            near[k, j].wait_recv()
-            forward(rows_in.at[tile, rows(peer(k)[1]), piece(j)], near_cross, j)
+        drain(some(j, half - direct), near_sem.at[j])
+        size = direct * cap
+        for b in range(1, half // direct):
+            begin = pl.multiple_of(block_of[b] * size, size)
+            forward(rows_in.at[tile, pl.ds(begin, size), piece(j)], near_cross, j)
 
     def relay(j):
         here = piece(j)
         if j == 0:
-            pending[0].wait_recv()
-        relayed[j].wait_recv()
+            drain(hot_in, table_sem.at[1, 0])
+        drain(relay_in.at[:, here], token_sem.at[j])
         relay_out[:, here] = jnp.dot(
             hot_in[...], relay_in[:, here], preferred_element_type=jnp.float32
         ).astype(jnp.bfloat16)
         for k in range(half - 1, 0, -1):
-            other, index = peer(k)
-            distant[k, j] = remote(
+            other, index = peers[k]
+            send(
                 relay_out.at[rows(index), here],
                 rows_in.at[tile, rows(h, span), here],
-                far_sem,
-                (k, j),
+                far_sem.at[n],
+                far_sem.at[j],
                 (other, tile),
             )
-            distant[k, j].start()
         rows_in[tile, rows(h, span), here] = relay_out[rows(h), here]
 
     def far_forward(j):
-        here = piece(j)
-        forward(rows_in.at[tile, rows(h, span), here], far_cross, j)
-        for k in range(1, half):
-            distant[k, j].wait_recv()
-            forward(rows_in.at[tile, rows(peer(k)[1], span), here], far_cross, j)
-
-    def near_passed(j):
-        return rows_in.at[0, pl.ds(0, (half - direct) * cap), piece(j)]
-
-    def far_passed(j):
-        return rows_in.at[0, pl.ds(0, span), piece(j)]
+        drain(some(j, half - 1), far_sem.at[j])
+        forward(rows_in.at[tile, span : 2 * span, piece(j)], far_cross, j)
 
     def consume(group, j):
         base = group * span
         if group == 0:
-            for k in range(1, direct):
-                near[k, j].wait_recv()
+            drain(many(j, direct - 1), direct_sem.at[j])
         for m in range(1, tiles):
             if group == 0:
-                drain(near_passed(j), near_cross, (1, m, j))
+                drain(some(j, half - direct), near_cross.at[m, j])
             else:
-                drain(far_passed(j), far_cross, (1, m, j))
+                drain(some(j, half), far_cross.at[m, j])
         if j == 0:
             gate[...] = jnp.zeros_like(gate)
             upward[...] = jnp.zeros_like(upward)
 
-        @pl.loop(0, tiles)
-        def _(m):
+        for m in range(tiles):
             block = rows_in[m, base : base + span, piece(j)]
             gate[...] += across(block, gate_w[:, columns(m, j)])
             upward[...] += across(block, up_w[:, columns(m, j)])
@@ -360,25 +348,21 @@
             hidden[group], down_w[:, columns(m, j)], preferred_element_type=jnp.float32
         )
 
-    home, tied = {}, {}
-
     def near_return(j):
         here = piece(j)
 
-        @pl.loop(0, tiles)
-        def _(m):
+        for m in range(tiles):
             near_answer[m, :, here] = project(0, m, j).astype(jnp.bfloat16)
 
         for k in range(half - 1, 0, -1):
-            other, index = peer(k)
-            home[k, j] = remote(
+            other, index = peers[k]
+            send(
                 near_answer.at[:, rows(index), here],
                 near_back.at[:, rows(h), here],
-                back_sem,
-                (k, j),
+                back_sem.at[n],
+                back_sem.at[j],
                 (other, tile),
             )
-            home[k, j].start()
         near_back[:, rows(h), here] = near_answer[:, rows(h), here]
 
     def blend(mix, block):
@@ -388,73 +372,67 @@
 
     def near_blend(j):
         here = piece(j)
-        for k in range(1, half):
-            home[k, j].wait_recv()
+        drain(many(j, half - 1), back_sem.at[j])
         for m in range(1, tiles):
             to = (tile + m) % tiles
             near_mixed[m - 1, :, here] = blend(near_mix, near_back[to, :, here]).astype(
                 jnp.bfloat16
             )
-            tied[m, j] = remote(
+            send(
                 near_mixed.at[m - 1, :, here],
                 mixed_in.at[m - 1, :, here],
-                mixed_sem,
-                (m, j),
+                mixed_sem.at[m, n],
+                mixed_sem.at[m, j],
                 (me, to),
             )
-            tied[m, j].start()
         own_mixed[:, here] = blend(near_mix, near_back[tile, :, here])
-
-    arrivals, others, sums = {}, {}, []
 
     def far_answer(j):
         here = piece(j)
         for m in range(1, tiles):
             to = (tile + m) % tiles
             answer[m - 1, :, here] = project(1, to, j).astype(jnp.bfloat16)
-            arrivals[m, j] = remote(
-                answer.at[m - 1, :, here], stage.at[m - 1, :, here], answer_sem, (m, j), (me, to)
-            )
-            arrivals[m, j].start()
+            send(
+                answer.at[m - 1, :, here],
+                stage.at[m - 1, :, here],
+                answer_sem.at[m, n],
+                answer_sem.at[m, j],
+                (me, to),
+            )
 
     def far_return(j):
         here = piece(j)
         total = project(1, tile, j)
         for m in range(1, tiles):
-            arrivals[m, j].wait_recv()
+            drain(stage.at[m - 1, :, here], answer_sem.at[m, j])
             total = total + stage[m - 1, :, here].astype(jnp.float32)
         reduced[:, here] = total.astype(jnp.bfloat16)
         for k in range(half - 1, 0, -1):
-            other, index = peer(k)
-            others[k, j] = remote(
+            other, index = peers[k]
+            send(
                 reduced.at[rows(index), here],
                 back.at[rows(h), here],
-                other_sem,
-                (k, j),
+                other_sem.at[n],
+                other_sem.at[j],
                 (other, tile),
             )
-            others[k, j].start()
         back[rows(h), here] = reduced[rows(h), here]
 
     def far_blend(j):
         here = piece(j)
         if j == 0:
-            pending[1].wait_recv()
-        for k in range(1, half):
-            others[k, j].wait_recv()
+            drain(mix_in, table_sem.at[1, 1])
+        drain(some(j, half - 1), other_sem.at[j])
         partial[:, here] = blend(mix_in, back[:, here]).astype(jnp.bfloat16)
-        sums.append(
-            remote(partial.at[:, here], summed.at[:, here], sum_sem, (j,), (far, tile))
-        )
-        sums[j].start()
+        send(partial.at[:, here], summed.at[:, here], sum_sem.at[n], sum_sem.at[j], (far, tile))
 
     def features(j):
         here = piece(j)
         mixed = own_mixed[:, here]
         for m in range(1, tiles):
-            tied[m, j].wait_recv()
+            drain(mixed_in.at[m - 1, :, here], mixed_sem.at[m, j])
             mixed = mixed + mixed_in[m - 1, :, here].astype(jnp.float32)
-        sums[j].wait_recv()
+        drain(summed.at[:, here], sum_sem.at[j])
         mixed = mixed + summed[:, here].astype(jnp.float32)
         feat = (tokens[tile, :, here].astype(jnp.float32) + mixed).astype(jnp.bfloat16)
         feat = feat.astype(jnp.float32)
@@ -503,8 +481,8 @@
         return total
 
     def earlier_frames():
-        for copy in pending[2:]:
-            copy.wait_recv()
+        for side in range(2):
+            drain(halo.at[side], halo_sem.at[1, side])
         left, right = shifts(tall)
         for t in range(2):
             top = halo[0, t].reshape(edge, channels)
@@ -551,8 +529,6 @@
             )
         out[...] = total.astype(jnp.bfloat16)
 
-    n = len(pieces)
-
     def steps(*stages):
         reach = n + max(lag for lag, _ in stages)
         for j in range(reach):
@@ -562,19 +538,36 @@
 
     for load in loads[1:3]:
         load.wait()
-    steps((0, near_forward), (1, functools.partial(consume, 0)))
+    late = max(n - 2, 0)
+    for j in range(n + 1):
+        if j < n:
+            relay(j)
+            near_forward(j)
+        if j >= 1:
+            consume(0, j - 1)
+        if 0 <= j - 2 < late:
+            far_forward(j - 2)
     activate(0)
-    steps((0, relay), (3, far_forward))
     loads[3].wait()
-    steps((0, near_return), (1, functools.partial(consume, 1)))
-    activate(1)
-    steps((0, far_answer))
-    steps((0, near_blend))
+    for j in turns:
+        near_return(j)
+        if late + j < n:
+            far_forward(late + j)
     for load in loads[4:]:
         load.wait()
     earlier_frames()
+    for j in turns:
+        consume(1, j)
+    activate(1)
+    for j in turns:
+        far_answer(j)
     found = []
-    steps((0, far_return), (1, far_blend), (2, lambda j: found.append(features(j))))
+    steps(
+        (0, far_return),
+        (0, near_blend),
+        (1, far_blend),
+        (2, lambda j: found.append(features(j))),
+    )
     square = sum(pair[0] for pair in found)
     coarse = sum(pair[1] for pair in found)
     lane = lax.broadcasted_iota(jnp.int32, (count, 128), 1)
@@ -583,30 +576,34 @@
     mine[:, channels:] = jnp.where(
         lane == 0, high, jnp.where(lane == 1, square - high, 0.0)
     ).astype(jnp.bfloat16)
-    totals = []
     for m in range(1, tiles):
-        totals.append(
-            remote(mine, theirs.at[m - 1], last_sem, (m,), (me, (tile + m) % tiles))
-        )
-        totals[-1].start()
-    for m, copy in enumerate(totals):
-        copy.wait_recv()
-        coarse = coarse + theirs[m, :, :channels].astype(jnp.float32)
+        send(mine, theirs.at[m - 1], last_sem.at[0, m], last_sem.at[1, m], (me, (tile + m) % tiles))
+    for m in range(1, tiles):
+        drain(theirs.at[m - 1], last_sem.at[1, m])
+        coarse = coarse + theirs[m - 1, :, :channels].astype(jnp.float32)
         square = square + jnp.sum(
-            theirs[m, :, channels:].astype(jnp.float32), axis=1, keepdims=True
+            theirs[m - 1, :, channels:].astype(jnp.float32), axis=1, keepdims=True
         )
     coarse_in[...] = coarse * lax.rsqrt(square * (1.0 / width) + epsilon)
     last_frame()
 
-    for copy in pending + relayed + sums + totals:
-        copy.wait_send()
-    for made in (near, distant, home, tied, others, arrivals):
-        for copy in made.values():
-            copy.wait_send()
-    for j in turns:
-        for m in range(1, tiles):
-            drain(near_passed(j), near_cross, (0, m, j))
-            drain(far_passed(j), far_cross, (0, m, j))
+    drain(far_hot, table_sem.at[0, 0])
+    drain(far_mix, table_sem.at[0, 1])
+    for side in range(2):
+        drain(halo.at[side], halo_sem.at[0, side])
+    drain(relay_in, token_sem.at[n])
+    drain(some(None, half - direct), near_sem.at[n])
+    drain(many(None, direct - 1), direct_sem.at[n])
+    drain(some(None, half - 1), far_sem.at[n])
+    drain(many(None, half - 1), back_sem.at[n])
+    drain(some(None, half - 1), other_sem.at[n])
+    drain(summed, sum_sem.at[n])
+    for m in range(1, tiles):
+        drain(some(None, half - direct), near_cross.at[m, n])
+        drain(some(None, half), far_cross.at[m, n])
+        drain(mixed_in.at[m - 1], mixed_sem.at[m, n])
+        drain(stage.at[m - 1], answer_sem.at[m, n])
+        drain(theirs.at[m - 1], last_sem.at[0, m])
 
 
 def layer(
@@ -691,16 +688,17 @@
         (12 + tiles,),
         (2, 2),
         (2, 2),
-        (2, n),
-        (2, half, n),
-        (2, half, n),
-        (2, tiles, n),
-        (2, tiles, n),
-        (2, half, n),
-        (2, tiles, n),
-        (2, tiles, n),
-        (2, half, n),
-        (2, n),
+        (n + 1,),
+        (n + 1,),
+        (n + 1,),
+        (n + 1,),
+        (tiles, n + 1),
+        (tiles, n + 1),
+        (n + 1,),
+        (tiles, n + 1),
+        (tiles, n + 1),
+        (n + 1,),
+        (n + 1,),
         (2, tiles),
     ]
     return pl.pallas_call(

time: 82 us -> 69.9 us (0.85)
  Pallas kernels: 79.7 us -> 67.6 us
    pallas_call x1, Pallas kernels: 79.7 us -> 67.6 us  [layer(): pl.pallas_call(functools.partial(layer_kernel, sessions, tiles, cap, piec...]
where the time goes in v3:
time: 69.9 us; the launch traced here: 69.8 us
  Pallas kernels  67.6 us (97%)
  local copies, waits for them, and re-layouts  1.47 us (2%)
    pallas_call x1, Pallas kernels, layer(): pl.pallas_call(functools.partial(layer_kernel, sessions, tiles, cap, piec...  67.6 us
    unnamed x1, local copies, waits for them, and re-layouts  1.47 us

profile of v3, /device:TPU:0, one launch (start us, length us, event | category | flops | bytes accessed | tf_op | source)
XLA Modules:
  0.0 69.8 jit_solution(1829636820635285482)
XLA Ops:
  0.7 67.6 %layer.1 = bf16[128,256]{1,0:T(8,128)(2,1)} custom-call(s32[2,64]{1,0:T(2,128)} %bitcast.30, f32[2,64]{1,0:T(2,128)} %bitcast.31, s32[1]{0:T(128)S(6)} %copy.16.head, f32[1,4096]{1,0:T(1,128)} %bitcast.29, bf16[64,4096]{1,0:T(8,128)(2,1)} %bitcast.26, bf16[704,4096]{1,0:T(8,128)(2,1)} %bitcast.21, bf16[704,4096]{1,0:T(8,128)(2,1)} %bitcast.22, ...), custom_call_target="tpu_custom_call" | custom-call | tf_op jit(solution)/shard_map/layer/pallas_call | solution.py:704
  68.3 1.5 %copy.17 = bf16[1,8,16,256]{3,2,1,0:T(8,128)(2,1)} copy(bf16[1,8,16,256]{3,2,1,0:T(8,128)(2,1)} %bitcast.27) | data formatting | bytes 131072

commit v4 on v3

--- a/solution.py
+++ b/solution.py
@@ -40,6 +40,10 @@
 def pieces_of(part):
     size = max(128, part // 4)
     return [(begin, size) for begin in range(0, part, size)]
+
+
+def fine_of(part, n):
+    return 2 if part // n % 256 == 0 else 1
 
 
 def layer_kernel(
@@ -136,6 +140,8 @@
     count, channels = tokens.shape[1], w_proj.shape[1]
     n = len(pieces)
     turns = range(n)
+    split = fine_of(part, n)
+    parts = range(n * split)
 
     def rows(index, base=0):
         return pl.ds(pl.multiple_of(base + index * cap, cap), cap)
@@ -150,6 +156,10 @@
     def columns(m, j):
         begin, size = pieces[j]
         return pl.ds(pl.multiple_of(m * part + begin, 128), size)
+
+    def fine(j):
+        size = part // len(parts)
+        return slice(j * size, (j + 1) * size)
 
     def send(source, target, sent, arrived, device):
         pltpu.make_async_remote_copy(
@@ -201,20 +211,6 @@
     for m in range(1, tiles):
         pl.semaphore_signal(
             barrier, inc=1, device_id=(me, (tile + m) % tiles), device_id_type=MESH
-        )
-
-    for load in token_loads[2:]:
-        load.wait()
-    pl.semaphore_wait(barrier, half + tiles - 1)
-
-    def hand_over(j):
-        here = piece(j)
-        send(
-            tokens.at[tile, :, here],
-            relay_in.at[:, here],
-            token_sem.at[n],
-            token_sem.at[j],
-            (far, tile),
         )
 
     token_loads[0].wait()
@@ -245,13 +241,40 @@
             weight = weight + jnp.where(hit, gates[k : k + 1, :], 0.0)
         hot[...] = onehot.astype(jnp.bfloat16)
         weights.append(weight)
+    for weight, mix in zip(weights, (near_mix, far_mix)):
+        weight = weight.T
+        high = weight.astype(jnp.bfloat16)
+        mix[0] = high
+        mix[1] = (weight - high.astype(jnp.float32)).astype(jnp.bfloat16)
+    for load in token_loads[2:]:
+        load.wait()
+    for j in turns:
+        for m in range(tiles):
+            near_out[m, :, piece(j)] = jnp.dot(
+                near_hot[...], tokens[m, :, piece(j)], preferred_element_type=jnp.float32
+            ).astype(jnp.bfloat16)
+    rows_in[:, rows(h), :] = near_out[:, rows(h), :]
+    loads[0].wait()
+    newest = head[0]
+    slots = [cache[i] for i in range(3)]
+    for t, shift in ((1, 0), (0, 2)):
+        which = lax.rem(newest + shift, 3)
+        past[t] = jnp.where(which == 0, slots[0], jnp.where(which == 1, slots[1], slots[2]))
+    pl.semaphore_wait(barrier, half + tiles - 1)
+
+    def hand_over(j):
+        here = piece(j)
+        send(
+            tokens.at[tile, :, here],
+            relay_in.at[:, here],
+            token_sem.at[n],
+            token_sem.at[j],
+            (far, tile),
+        )
+
     send(far_hot, hot_in, table_sem.at[0, 0], table_sem.at[1, 0], (far, tile))
     for j in turns:
         here = piece(j)
-        for m in range(tiles):
-            near_out[m, :, here] = jnp.dot(
-                near_hot[...], tokens[m, :, here], preferred_element_type=jnp.float32
-            ).astype(jnp.bfloat16)
         for k in range(half - 1, 0, -1):
             other, index = peers[k]
             if k < direct:
@@ -262,22 +285,10 @@
                 target = rows_in.at[tile, rows(h), here]
                 sems = near_sem
             send(source, target, sems.at[n], sems.at[j], (other, tile))
-        rows_in[:, rows(h), here] = near_out[:, rows(h), here]
     for j in turns:
         hand_over(j)
-    for weight, mix in zip(weights, (near_mix, far_mix)):
-        weight = weight.T
-        high = weight.astype(jnp.bfloat16)
-        mix[0] = high
-        mix[1] = (weight - high.astype(jnp.float32)).astype(jnp.bfloat16)
     send(far_mix, mix_in, table_sem.at[0, 1], table_sem.at[1, 1], (far, tile))
 
-    loads[0].wait()
-    newest = head[0]
-    slots = [cache[i] for i in range(3)]
-    for t, shift in ((1, 0), (0, 2)):
-        which = lax.rem(newest + shift, 3)
-        past[t] = jnp.where(which == 0, slots[0], jnp.where(which == 1, slots[1], slots[2]))
     height = past.shape[1]
     for side, start, step in ((0, height - HALO, 1), (1, 0, tiles - 1)):
         send(
@@ -343,16 +354,15 @@
     def activate(group):
         hidden[group] = (silu(gate[...]) * upward[...]).astype(jnp.bfloat16)
 
-    def project(group, m, j):
-        return jnp.dot(
-            hidden[group], down_w[:, columns(m, j)], preferred_element_type=jnp.float32
-        )
+    def project(group, m, here):
+        span_in = pl.ds(pl.multiple_of(m * part + here.start, 128), here.stop - here.start)
+        return jnp.dot(hidden[group], down_w[:, span_in], preferred_element_type=jnp.float32)
 
     def near_return(j):
         here = piece(j)
 
         for m in range(tiles):
-            near_answer[m, :, here] = project(0, m, j).astype(jnp.bfloat16)
+            near_answer[m, :, here] = project(0, m, here).astype(jnp.bfloat16)
 
         for k in range(half - 1, 0, -1):
             other, index = peers[k]
@@ -388,21 +398,21 @@
         own_mixed[:, here] = blend(near_mix, near_back[tile, :, here])
 
     def far_answer(j):
-        here = piece(j)
+        here = fine(j)
         for m in range(1, tiles):
             to = (tile + m) % tiles
-            answer[m - 1, :, here] = project(1, to, j).astype(jnp.bfloat16)
+            answer[m - 1, :, here] = project(1, to, here).astype(jnp.bfloat16)
             send(
                 answer.at[m - 1, :, here],
                 stage.at[m - 1, :, here],
-                answer_sem.at[m, n],
+                answer_sem.at[m, n * split],
                 answer_sem.at[m, j],
                 (me, to),
             )
 
     def far_return(j):
-        here = piece(j)
-        total = project(1, tile, j)
+        here = fine(j)
+        total = project(1, tile, here)
         for m in range(1, tiles):
             drain(stage.at[m - 1, :, here], answer_sem.at[m, j])
             total = total + stage[m - 1, :, here].astype(jnp.float32)
@@ -412,25 +422,27 @@
             send(
                 reduced.at[rows(index), here],
                 back.at[rows(h), here],
-                other_sem.at[n],
+                other_sem.at[n * split],
                 other_sem.at[j],
                 (other, tile),
             )
         back[rows(h), here] = reduced[rows(h), here]
 
     def far_blend(j):
-        here = piece(j)
+        here = fine(j)
         if j == 0:
             drain(mix_in, table_sem.at[1, 1])
-        drain(some(j, half - 1), other_sem.at[j])
+        drain(rows_in.at[0, pl.ds(0, (half - 1) * cap), here], other_sem.at[j])
         partial[:, here] = blend(mix_in, back[:, here]).astype(jnp.bfloat16)
-        send(partial.at[:, here], summed.at[:, here], sum_sem.at[n], sum_sem.at[j], (far, tile))
+        send(partial.at[:, here], summed.at[:, here], sum_sem.at[n * split], sum_sem.at[j], (far, tile))
 
     def features(j):
-        here = piece(j)
+        here = fine(j)
         mixed = own_mixed[:, here]
         for m in range(1, tiles):
-            drain(mixed_in.at[m - 1, :, here], mixed_sem.at[m, j])
+            if j % split == 0:
+                whole = piece(j // split)
+                drain(mixed_in.at[m - 1, :, whole], mixed_sem.at[m, j // split])
             mixed = mixed + mixed_in[m - 1, :, here].astype(jnp.float32)
         drain(summed.at[:, here], sum_sem.at[j])
         mixed = mixed + summed[:, here].astype(jnp.float32)
@@ -529,45 +541,38 @@
             )
         out[...] = total.astype(jnp.bfloat16)
 
-    def steps(*stages):
-        reach = n + max(lag for lag, _ in stages)
-        for j in range(reach):
-            for lag, stage_of in stages:
-                if 0 <= j - lag < n:
-                    stage_of(j - lag)
-
     for load in loads[1:3]:
         load.wait()
-    late = max(n - 2, 0)
-    for j in range(n + 1):
+    for j in range(n + 3):
         if j < n:
             relay(j)
             near_forward(j)
-        if j >= 1:
-            consume(0, j - 1)
-        if 0 <= j - 2 < late:
-            far_forward(j - 2)
+        if 0 <= j - 2 < n:
+            consume(0, j - 2)
+        if 0 <= j - 3:
+            far_forward(j - 3)
     activate(0)
     loads[3].wait()
     for j in turns:
         near_return(j)
-        if late + j < n:
-            far_forward(late + j)
     for load in loads[4:]:
         load.wait()
     earlier_frames()
     for j in turns:
         consume(1, j)
     activate(1)
-    for j in turns:
+    for j in parts:
         far_answer(j)
     found = []
-    steps(
-        (0, far_return),
-        (0, near_blend),
-        (1, far_blend),
-        (2, lambda j: found.append(features(j))),
-    )
+    for j in range(len(parts) + 6):
+        if j < len(parts):
+            far_return(j)
+            if j % split == 0:
+                near_blend(j // split)
+        if 0 <= j - 2 < len(parts):
+            far_blend(j - 2)
+        if 0 <= j - 6:
+            found.append(features(j - 6))
     square = sum(pair[0] for pair in found)
     coarse = sum(pair[1] for pair in found)
     lane = lax.broadcasted_iota(jnp.int32, (count, 128), 1)
@@ -596,13 +601,13 @@
     drain(many(None, direct - 1), direct_sem.at[n])
     drain(some(None, half - 1), far_sem.at[n])
     drain(many(None, half - 1), back_sem.at[n])
-    drain(some(None, half - 1), other_sem.at[n])
-    drain(summed, sum_sem.at[n])
+    drain(some(None, half - 1), other_sem.at[n * split])
+    drain(summed, sum_sem.at[n * split])
     for m in range(1, tiles):
         drain(some(None, half - direct), near_cross.at[m, n])
         drain(some(None, half), far_cross.at[m, n])
         drain(mixed_in.at[m - 1], mixed_sem.at[m, n])
-        drain(stage.at[m - 1], answer_sem.at[m, n])
+        drain(stage.at[m - 1], answer_sem.at[m, n * split])
         drain(theirs.at[m - 1], last_sem.at[0, m])
 
 
@@ -635,6 +640,7 @@
     hbm = pl.BlockSpec(memory_space=pltpu.HBM)
     low, full = jnp.bfloat16, jnp.float32
     n = len(pieces)
+    split = fine_of(part, n)
     held = [
         (routes.shape, routes.dtype),
         (gates.shape, full),
@@ -696,9 +702,9 @@
         (tiles, n + 1),
         (n + 1,),
         (tiles, n + 1),
-        (tiles, n + 1),
-        (n + 1,),
-        (n + 1,),
+        (tiles, n * split + 1),
+        (n * split + 1,),
+        (n * split + 1,),
         (2, tiles),
     ]
     return pl.pallas_call(

time: 69.9 us -> 67.4 us (0.964)
  Pallas kernels: 67.6 us -> 65.1 us
    pallas_call x1, Pallas kernels: 67.6 us -> 65.1 us  [layer(): pl.pallas_call(functools.partial(layer_kernel, sessions, tiles, cap, piec...]
where the time goes in v4:
time: 67.4 us; the launch traced here: 67.3 us
  Pallas kernels  65.1 us (97%)
  local copies, waits for them, and re-layouts  1.47 us (2%)
    pallas_call x1, Pallas kernels, layer(): pl.pallas_call(functools.partial(layer_kernel, sessions, tiles, cap, piec...  65.1 us
    unnamed x1, local copies, waits for them, and re-layouts  1.47 us

profile of v4, /device:TPU:0, one launch (start us, length us, event | category | flops | bytes accessed | tf_op | source)
XLA Modules:
  0.0 67.3 jit_solution(6180319752474164654)
XLA Ops:
  0.7 65.1 %layer.1 = bf16[128,256]{1,0:T(8,128)(2,1)} custom-call(s32[2,64]{1,0:T(2,128)} %bitcast.30, f32[2,64]{1,0:T(2,128)} %bitcast.31, s32[1]{0:T(128)S(6)} %copy.16.head, f32[1,4096]{1,0:T(1,128)} %bitcast.29, bf16[64,4096]{1,0:T(8,128)(2,1)} %bitcast.26, bf16[704,4096]{1,0:T(8,128)(2,1)} %bitcast.21, bf16[704,4096]{1,0:T(8,128)(2,1)} %bitcast.22, ...), custom_call_target="tpu_custom_call" | custom-call | tf_op jit(solution)/shard_map/layer/pallas_call | solution.py:710
  65.8 1.5 %copy.17 = bf16[1,8,16,256]{3,2,1,0:T(8,128)(2,1)} copy(bf16[1,8,16,256]{3,2,1,0:T(8,128)(2,1)} %bitcast.27) | data formatting | bytes 131072

commit v5 on v4

--- a/solution.py
+++ b/solution.py
@@ -543,36 +543,37 @@
 
     for load in loads[1:3]:
         load.wait()
-    for j in range(n + 3):
-        if j < n:
-            relay(j)
-            near_forward(j)
-        if 0 <= j - 2 < n:
-            consume(0, j - 2)
-        if 0 <= j - 3:
-            far_forward(j - 3)
+    for j in turns:
+        near_forward(j)
+        relay(j)
+    for j in turns:
+        if j < n - 1:
+            far_forward(j)
+        consume(0, j)
     activate(0)
     loads[3].wait()
     for j in turns:
         near_return(j)
+        if j == 0:
+            far_forward(n - 1)
     for load in loads[4:]:
         load.wait()
-    earlier_frames()
     for j in turns:
         consume(1, j)
     activate(1)
     for j in parts:
         far_answer(j)
+    earlier_frames()
     found = []
-    for j in range(len(parts) + 6):
+    for j in range(len(parts) + 7):
         if j < len(parts):
             far_return(j)
             if j % split == 0:
                 near_blend(j // split)
         if 0 <= j - 2 < len(parts):
             far_blend(j - 2)
-        if 0 <= j - 6:
-            found.append(features(j - 6))
+        if 0 <= j - 7:
+            found.append(features(j - 7))
     square = sum(pair[0] for pair in found)
     coarse = sum(pair[1] for pair in found)
     lane = lax.broadcasted_iota(jnp.int32, (count, 128), 1)

time: 67.4 us -> 66.1 us (0.981)
  Pallas kernels: 65.1 us -> 63.8 us
    pallas_call x1, Pallas kernels: 65.1 us -> 63.8 us  [layer(): pl.pallas_call(functools.partial(layer_kernel, sessions, tiles, cap, piec...]
where the time goes in v5:
time: 66.1 us; the launch traced here: 66 us
  Pallas kernels  63.8 us (97%)
  local copies, waits for them, and re-layouts  1.47 us (2%)
    pallas_call x1, Pallas kernels, layer(): pl.pallas_call(functools.partial(layer_kernel, sessions, tiles, cap, piec...  63.8 us
    unnamed x1, local copies, waits for them, and re-layouts  1.47 us

profile of v5, /device:TPU:0, one launch (start us, length us, event | category | flops | bytes accessed | tf_op | source)
XLA Modules:
  0.0 66.0 jit_solution(8550790444702518284)
XLA Ops:
  0.7 63.8 %layer.1 = bf16[128,256]{1,0:T(8,128)(2,1)} custom-call(s32[2,64]{1,0:T(2,128)} %bitcast.30, f32[2,64]{1,0:T(2,128)} %bitcast.31, s32[1]{0:T(128)S(6)} %copy.16.head, f32[1,4096]{1,0:T(1,128)} %bitcast.29, bf16[64,4096]{1,0:T(8,128)(2,1)} %bitcast.26, bf16[704,4096]{1,0:T(8,128)(2,1)} %bitcast.21, bf16[704,4096]{1,0:T(8,128)(2,1)} %bitcast.22, ...), custom_call_target="tpu_custom_call" | custom-call | tf_op jit(solution)/shard_map/layer/pallas_call | solution.py:711
  64.5 1.5 %copy.17 = bf16[1,8,16,256]{3,2,1,0:T(8,128)(2,1)} copy(bf16[1,8,16,256]{3,2,1,0:T(8,128)(2,1)} %bitcast.27) | data formatting | bytes 131072
